TPU v7x, 1024 devices: a whole 4x8x16 slice. The times are simulated.
1024 devices in a mesh: col: 64 (over y, x, core), grp: 16 (over z).
Axes of the slice: x: 4, y: 8, z: 16, core: 2. Of those that a mesh axis runs over, the one named last changes fastest.
Arguments:
- profiles: float32 [16384, 116], P('col'), may hold values from -6 to 6
- courant: float32 [16384, 58], P('col'), may hold values from -0.7 to 0.7
- owner_map: int32 [16384], replicated, may hold values from 0 to 16383, as said below
- cloud_flags: int32 [16384], P('col'), may hold values 0 or 1
- crm_state: float32 [2, 58, 64, 16384], P(None, None, 'grp', 'col'), may hold values from -6 to 6
Outputs:
- tendency: float32 [16384, 116], P('col')
- crm_final: float32 [2, 58, 64, 16384], P(None, None, 'grp', 'col')
Inputs may be any that keep to these rules, and one draw needn't show every extreme that they name: owner_map is a permutation; physics column p lives in span p // 256, element column e in group e // 256; each group hands at most 6 columns to one span, and exactly 6 to some spans, and every span receives exactly 256 columns.
All inputs are finite; a program needn't handle non-finite values. No bound on the sum of `cloud_flags` on one device may be relied on, other than what follows from the above.
Results may differ from a plain program's by a relative error of at most 0.00002.
Values sent between devices are 32-bit elements; how exact they have to be, the bound alone decides.
No kernel may reach another device: no remote copies, remote signals or barrier semaphores. Data moves between devices by JAX's collectives and lax.ppermute only.
A program may use at most 32 MiB of HBM per device.

v0:
```python
import jax
import jax.numpy as jnp
from jax import lax
from jax.sharding import PartitionSpec as P

STEPS = 8


diffuse_x = 0.25
diffuse_z = 0.2
sat_scale = 0.5
sat_slope = 0.3
cond_rate = 0.5
latent_gain = 0.4


def sent_together(arrays, axis, split_dim, concat_dim, along):
    ends, at = ([], 0)
    for a in arrays[:-1]:
        at += a.shape[along]
        ends.append(at)
    both = jnp.concatenate(arrays, axis=along)
    return tuple(
        jnp.split(
            lax.all_to_all(both, axis, split_axis=split_dim, concat_axis=concat_dim, tiled=True),
            ends,
            axis=along,
        )
    )


def padded(x, sides, width):
    for axis, dim in sides:
        peers, length = (lax.axis_size(axis), x.shape[dim])
        up = [(i, (i + 1) % peers) for i in range(peers)]
        down = [(j, i) for i, j in up]
        last = lax.slice_in_dim(x, length - width, length, axis=dim)
        leading = lax.slice_in_dim(x, 0, width, axis=dim)
        before = lax.ppermute(last, axis, up)
        after = lax.ppermute(leading, axis, down)
        x = jnp.concatenate([before, x, after], axis=dim)
    return x


def over_pieces(x, axis):
    return lax.all_gather(x, axis).sum(0)


def condense(fields, cloudy):
    energy = fields[0]
    moisture = fields[1]
    saturation = sat_scale * (jnp.exp(sat_slope * energy) - 1.0)
    amount = cond_rate * jnp.maximum(moisture - saturation, 0.0) * cloudy
    return jnp.stack([energy + latent_gain * amount, moisture - amount])


def advance(widened, courant_here, forcing, cloudy):
    centre = widened[:, :, 1:-1]
    eastern = widened[:, :, 2:]
    western = widened[:, :, :-2]
    upper = jnp.concatenate([centre[:, 1:], centre[:, -1:]], axis=1)
    lower = jnp.concatenate([centre[:, :1], centre[:, :-1]], axis=1)
    stepped = (
        centre
        + courant_here * ((western - eastern) * 0.5)
        + diffuse_x * (eastern - 2.0 * centre + western)
        + diffuse_z * (upper - 2.0 * centre + lower)
        + forcing
    )
    return condense(stepped, cloudy)


def on_device(profiles, courant, owner_map, cloud_flags, crm_state):
    columns = profiles.shape[0]
    levels = courant.shape[1]
    col_count = lax.axis_size("col")
    col_index = lax.axis_index("col")
    per_peer = columns // col_count
    capacity = per_peer + min(2, per_peer)
    positions = jnp.arange(columns, dtype=jnp.int32)
    my_owner = lax.dynamic_slice_in_dim(owner_map, col_index * columns, columns)
    target = my_owner // columns
    earlier = (target[:, None] == target[None, :]) & (positions[None, :] < positions[:, None])
    order_in = jnp.sum(earlier.astype(jnp.int32), axis=1)
    sent_slot = target * capacity + order_in
    send_rows = jnp.full((col_count * capacity,), columns, jnp.int32).at[sent_slot].set(positions)
    padded_prof = jnp.concatenate([profiles, jnp.zeros((1, profiles.shape[1]), jnp.float32)])
    padded_cour = jnp.concatenate([courant, jnp.zeros((1, levels), jnp.float32)])
    out_prof = padded_prof[send_rows].reshape(col_count, capacity, profiles.shape[1])
    out_cour = padded_cour[send_rows].reshape(col_count, capacity, levels)
    got_prof, got_cour = sent_together((out_prof, out_cour), "col", 0, 0, 2)
    block_view = owner_map.reshape(col_count, columns)
    landing = (block_view // columns == col_index).astype(jnp.int32)
    before = jnp.cumsum(landing, axis=1) - landing
    sources = jnp.arange(col_count, dtype=jnp.int32)[:, None]
    where_from = sources * capacity + before
    landing_slot = jnp.where(landing > 0, block_view - col_index * columns, columns)
    senders_block = 4
    slot_blocks = landing_slot.reshape(col_count // senders_block, senders_block * columns)
    from_blocks = where_from.reshape(col_count // senders_block, senders_block * columns)

    def match_block(found, pair):
        slots, anchors = pair
        hits = slots[None, :] == positions[:, None]
        return (found + jnp.sum(jnp.where(hits, anchors[None, :], 0), axis=1), None)

    take_rows, unused = lax.scan(
        match_block, jnp.zeros((columns,), jnp.int32), (slot_blocks, from_blocks)
    )
    phys_prof = got_prof.reshape(col_count * capacity, profiles.shape[1])[take_rows]
    phys_cour = got_cour.reshape(col_count * capacity, levels)[take_rows]
    forcing = (phys_prof.reshape(columns, 2, levels).transpose(1, 2, 0) / STEPS)[:, :, None, :]
    courant_here = phys_cour.T[None, :, None, :]
    cloudy = cloud_flags.astype(jnp.float32)
    crm_now = crm_state
    for repeat in range(STEPS // 2):
        widened = padded(crm_now, (("grp", 2),), 2)
        middle = advance(widened, courant_here, forcing, cloudy)
        crm_now = advance(middle, courant_here, forcing, cloudy)
    cells_all = crm_state.shape[2] * lax.axis_size("grp")
    partial_value = jnp.sum(crm_now, axis=2) - jnp.sum(crm_state, axis=2)
    totals = over_pieces(partial_value, "grp")
    increment = totals / cells_all
    phys_inc = increment.transpose(2, 0, 1).reshape(columns, 2 * levels)
    back_rows = (
        jnp.zeros((col_count * capacity, 2 * levels), jnp.float32).at[take_rows].set(phys_inc)
    )
    got_back = lax.all_to_all(
        back_rows.reshape(col_count, capacity, 2 * levels),
        "col",
        split_axis=0,
        concat_axis=0,
        tiled=True,
    )
    tendency = got_back.reshape(col_count * capacity, 2 * levels)[sent_slot]
    return (tendency, crm_now)


def solution(mesh):
    placed = (P("col", None), P("col", None), P(), P("col"), P(None, None, "grp", "col"))
    return jax.shard_map(
        on_device,
        mesh=mesh,
        in_specs=placed,
        out_specs=(P("col", None), P(None, None, "grp", "col")),
        check_vma=False,
    )
```

profile of v0, /device:TPU:1, one launch (start us, length us, event | category | flops | bytes accessed | tf_op | source)
XLA Modules:
  0.0 213.2 jit_solution(10140408004635947155)
XLA Ops:
  7.2 0.8 and_select_fusion
  8.2 0.8 compare_select_fusion.1
  8.9 1.4 scatter_custom_fusion
  10.4 1.0 copy.54
  11.4 1.1 gather_fusion
  12.7 1.1 gather_fusion.1
  13.9 1.0 pad_maximum_fusion.9
  14.9 18.3 %all-to-all-start = ((f32[64,6,174]{2,1,0:T(8,128)}), f32[64,6,174]{2,1,0:T(8,128)S(1)}, u32[]{:S(2)}, u32[]{:S(2)}) async-start(f32[64,6,174]{2,1,0:T(8,128)} %pad_maximum_fusion.9), calls=%async_computation | async-start | bytes 1048576 | tf_op jit(solution)/shard_map/all_to_all | solution.py:25
  33.5 1.9 collective-permute-start
  35.4 11.4 %collective-permute-start.1 = (f32[2,58,2,256]{3,2,1,0:T(2,128)S(1)}, f32[2,58,2,256]{3,2,1,0:T(2,128)S(1)}, u32[]{:S(2)}, u32[]{:S(2)}) collective-permute-start(f32[2,58,2,256]{3,2,1,0:T(2,128)S(1)} %get-tuple-element.109), channel_id=1, source_target_pairs={{1,0},{2,1},{3,2},{4,3},{5,4},{6,5},{7,6},{8,7},{9,8},{10,9},{11,1... | collective-permute-start | bytes 712712 | tf_op jit(solution)/shard_map/ppermute | solution.py:40
  46.9 0.6 reduce-window.6
  48.1 3.9 %while.11 = (s32[]{:T(128)}, s32[256]{0:T(256)S(1)}, s32[16,1024]{1,0:T(8,128)S(1)}, s32[16,1024]{1,0:T(8,128)S(1)}, s32[]{:T(128)}, /*index=5*/s32[]{:T(128)}) while((s32[]{:T(128)}, s32[256]{0:T(256)S(1)}, s32[16,1024]{1,0:T(8,128)S(1)}, s32[16,1024]{1,0:T(8,128)S(1)}, s32[]{:T(128)}, /*index=5*/s32[]{:T(128)}) %tuple.57), condition=%wide.region_4.5_spmd.clone, body=%wide.region_2.4_spmd.clone.sunk | while | flops 786691 | bytes 28755 | solution.py:107
  52.1 0.7 copy-done.1
  52.8 0.7 copy-done.3
  53.5 0.3 pad_maximum_fusion
  53.8 1.1 fusion.120
  54.9 0.7 gather_fusion.3
  56.0 0.7 gather_fusion.2
  56.9 2.1 fusion.9
  59.4 0.6 fusion.83
  60.4 1.9 collective-permute-start.2
  62.3 7.4 %collective-permute-start.3 = (f32[2,58,2,256]{3,2,1,0:T(2,128)S(1)}, f32[2,58,2,256]{3,2,1,0:T(2,128)S(1)}, u32[]{:S(2)}, u32[]{:S(2)}) collective-permute-start(f32[2,58,2,256]{3,2,1,0:T(2,128)S(1)} %get-tuple-element.107), channel_id=1, source_target_pairs={{1,0},{2,1},{3,2},{4,3},{5,4},{6,5},{7,6},{8,7},{9,8},{10,9},{11,1... | collective-permute-start | bytes 712712 | tf_op jit(solution)/shard_map/ppermute | solution.py:40
  69.7 3.8 %collective-permute-done.2 = f32[2,58,2,256]{3,2,1,0:T(2,128)S(1)} collective-permute-done((f32[2,58,2,256]{3,2,1,0:T(2,128)S(1)}, f32[2,58,2,256]{3,2,1,0:T(2,128)S(1)}, u32[]{:S(2)}, u32[]{:S(2)}) %collective-permute-start.2) | collective-permute-done | bytes 237600 | tf_op jit(solution)/shard_map/ppermute | solution.py:39
  73.6 0.9 collective-permute-done.3
  74.9 0.9 fusion.21
  76.2 0.6 fusion.78
  77.2 1.9 collective-permute-start.4
  79.1 5.5 %collective-permute-start.5 = (f32[2,58,2,256]{3,2,1,0:T(2,128)S(1)}, f32[2,58,2,256]{3,2,1,0:T(2,128)S(1)}, u32[]{:S(2)}, u32[]{:S(2)}) collective-permute-start(f32[2,58,2,256]{3,2,1,0:T(2,128)S(1)} %get-tuple-element.105), channel_id=1, source_target_pairs={{1,0},{2,1},{3,2},{4,3},{5,4},{6,5},{7,6},{8,7},{9,8},{10,9},{11,1... | collective-permute-start | bytes 712712 | tf_op jit(solution)/shard_map/ppermute | solution.py:40
  84.6 2.8 %collective-permute-done.4 = f32[2,58,2,256]{3,2,1,0:T(2,128)S(1)} collective-permute-done((f32[2,58,2,256]{3,2,1,0:T(2,128)S(1)}, f32[2,58,2,256]{3,2,1,0:T(2,128)S(1)}, u32[]{:S(2)}, u32[]{:S(2)}) %collective-permute-start.4) | collective-permute-done | bytes 237600 | tf_op jit(solution)/shard_map/ppermute | solution.py:39
  87.4 0.9 collective-permute-done.5
  88.8 0.9 fusion.34
  90.0 0.6 fusion.73
  91.0 1.9 collective-permute-start.6
  93.0 5.3 %collective-permute-start.7 = (f32[2,58,2,256]{3,2,1,0:T(2,128)S(1)}, f32[2,58,2,256]{3,2,1,0:T(2,128)S(1)}, u32[]{:S(2)}, u32[]{:S(2)}) collective-permute-start(f32[2,58,2,256]{3,2,1,0:T(2,128)S(1)} %get-tuple-element.103), channel_id=1, source_target_pairs={{1,0},{2,1},{3,2},{4,3},{5,4},{6,5},{7,6},{8,7},{9,8},{10,9},{11,1... | collective-permute-start | bytes 712712 | tf_op jit(solution)/shard_map/ppermute | solution.py:40
  98.6 1.8 collective-permute-done.6
  100.4 0.9 collective-permute-done.7
  101.8 0.9 fusion.47
  103.1 0.6 fusion.68
  103.9 0.9 fusion.116
  104.8 0.7 sub.260
  105.5 62.7 %all-gather.3.cloned.1.call-done = f32[32,58,256]{2,1,0:T(8,128)} async-done(((f32[2,58,256]{2,1,0:T(8,128)}), f32[32,58,256]{2,1,0:T(8,128)}) %all-gather.3.cloned.1.call-update) | async-done | bytes 1900560 | tf_op jit(solution)/shard_map/all_gather | solution.py:46
  168.2 1.7 reduce_sum.48
  170.0 1.2 scatter_custom_fusion.1
  171.2 0.7 reshape.90
  172.0 19.8 %all-to-all-start.1 = ((f32[64,6,116]{2,1,0:T(8,128)}), f32[64,6,116]{2,1,0:T(8,128)S(1)}, u32[]{:S(2)}, u32[]{:S(2)}) async-start(f32[64,6,116]{2,1,0:T(8,128)} %reshape.90), calls=%async_computation.1 | async-start | bytes 524288 | tf_op jit(solution)/shard_map/all_to_all | solution.py:128
  191.8 13.1 %all-to-all-done.1 = f32[64,6,116]{2,1,0:T(8,128)S(1)} async-done(((f32[64,6,116]{2,1,0:T(8,128)}), f32[64,6,116]{2,1,0:T(8,128)S(1)}, u32[]{:S(2)}, u32[]{:S(2)}) %all-to-all-start.1) | async-done | bytes 178208 | tf_op jit(solution)/shard_map/all_to_all | solution.py:128
  204.9 0.7 gather_fusion.4
  205.6 0.8 copy.60
  (133 shorter events, 9.8 us)
Async XLA Ops:
  7.2 5.4 %copy-start.6 = (f32[256,58]{0,1:T(8,128)S(1)}, f32[256,58]{0,1:T(8,128)}, u32[]{:S(2)}) copy-start(f32[256,58]{0,1:T(8,128)} %param.8) | copy-start | bytes 178180
  12.7 20.6 %copy-start = (f32[2,58,4,256]{3,2,1,0:T(4,128)S(1)}, f32[2,58,4,256]{3,2,1,0:T(4,128)}, u32[]{:S(2)}) copy-start(f32[2,58,4,256]{3,2,1,0:T(4,128)} %param.11) | copy-start | bytes 1425412
  13.8 33.0 %copy-start.5 = (s32[16384]{0:T(1024)S(1)}, s32[16384]{0:T(1024)}, u32[]{:S(2)}) copy-start(s32[16384]{0:T(1024)} %param.9) | copy-start | bytes 196612
  14.9 37.1 %copy-start.7 = (s32[256]{0:T(256)S(1)}, s32[256]{0:T(256)}, u32[]{:S(2)}) copy-start(s32[256]{0:T(256)} %param.10) | copy-start | bytes 3076
  14.9 40.0 %all-to-all-start = ((f32[64,6,174]{2,1,0:T(8,128)}), f32[64,6,174]{2,1,0:T(8,128)S(1)}, u32[]{:S(2)}, u32[]{:S(2)}) async-start(f32[64,6,174]{2,1,0:T(8,128)} %pad_maximum_fusion.9), calls=%async_computation | async-start | bytes 1048576 | tf_op jit(solution)/shard_map/all_to_all | solution.py:25
  33.2 134.9 %all-gather.3.cloned.1.call-start = ((), (), s32[]{:S(2)}) async-start(), calls=%async_computation.2 | async-start | bytes 2228224 | tf_op jit(solution)/shard_map/all_gather | solution.py:46
  33.5 18.6 %collective-permute-start = (f32[2,58,2,256]{3,2,1,0:T(2,128)S(1)}, f32[2,58,2,256]{3,2,1,0:T(2,128)S(1)}, u32[]{:S(2)}, u32[]{:S(2)}) collective-permute-start(f32[2,58,2,256]{3,2,1,0:T(2,128)S(1)} %get-tuple-element.110), channel_id=1, source_target_pairs={{0,1},{1,2},{2,3},{3,4},{4,5},{5,6},{6,7},{7,8},{8,9},{9,10},{10,1... | collective-permute-start | bytes 712712 | tf_op jit(solution)/shard_map/ppermute | solution.py:39
  35.4 16.7 %collective-permute-start.1 = (f32[2,58,2,256]{3,2,1,0:T(2,128)S(1)}, f32[2,58,2,256]{3,2,1,0:T(2,128)S(1)}, u32[]{:S(2)}, u32[]{:S(2)}) collective-permute-start(f32[2,58,2,256]{3,2,1,0:T(2,128)S(1)} %get-tuple-element.109), channel_id=1, source_target_pairs={{1,0},{2,1},{3,2},{4,3},{5,4},{6,5},{7,6},{8,7},{9,8},{10,9},{11,1... | collective-permute-start | bytes 712712 | tf_op jit(solution)/shard_map/ppermute | solution.py:40
  52.1 0.7 copy-start.1
  52.8 0.7 copy-start.3
  55.7 1.2 copy-start.4
  55.9 1.0 copy-start.2
  60.4 13.2 %collective-permute-start.2 = (f32[2,58,2,256]{3,2,1,0:T(2,128)S(1)}, f32[2,58,2,256]{3,2,1,0:T(2,128)S(1)}, u32[]{:S(2)}, u32[]{:S(2)}) collective-permute-start(f32[2,58,2,256]{3,2,1,0:T(2,128)S(1)} %get-tuple-element.108), channel_id=1, source_target_pairs={{0,1},{1,2},{2,3},{3,4},{4,5},{5,6},{6,7},{7,8},{8,9},{9,10},{10,1... | collective-permute-start | bytes 712712 | tf_op jit(solution)/shard_map/ppermute | solution.py:39
  62.3 12.1 %collective-permute-start.3 = (f32[2,58,2,256]{3,2,1,0:T(2,128)S(1)}, f32[2,58,2,256]{3,2,1,0:T(2,128)S(1)}, u32[]{:S(2)}, u32[]{:S(2)}) collective-permute-start(f32[2,58,2,256]{3,2,1,0:T(2,128)S(1)} %get-tuple-element.107), channel_id=1, source_target_pairs={{1,0},{2,1},{3,2},{4,3},{5,4},{6,5},{7,6},{8,7},{9,8},{10,9},{11,1... | collective-permute-start | bytes 712712 | tf_op jit(solution)/shard_map/ppermute | solution.py:40
  77.2 10.2 %collective-permute-start.4 = (f32[2,58,2,256]{3,2,1,0:T(2,128)S(1)}, f32[2,58,2,256]{3,2,1,0:T(2,128)S(1)}, u32[]{:S(2)}, u32[]{:S(2)}) collective-permute-start(f32[2,58,2,256]{3,2,1,0:T(2,128)S(1)} %get-tuple-element.106), channel_id=1, source_target_pairs={{0,1},{1,2},{2,3},{3,4},{4,5},{5,6},{6,7},{7,8},{8,9},{9,10},{10,1... | collective-permute-start | bytes 712712 | tf_op jit(solution)/shard_map/ppermute | solution.py:39
  79.1 9.2 %collective-permute-start.5 = (f32[2,58,2,256]{3,2,1,0:T(2,128)S(1)}, f32[2,58,2,256]{3,2,1,0:T(2,128)S(1)}, u32[]{:S(2)}, u32[]{:S(2)}) collective-permute-start(f32[2,58,2,256]{3,2,1,0:T(2,128)S(1)} %get-tuple-element.105), channel_id=1, source_target_pairs={{1,0},{2,1},{3,2},{4,3},{5,4},{6,5},{7,6},{8,7},{9,8},{10,9},{11,1... | collective-permute-start | bytes 712712 | tf_op jit(solution)/shard_map/ppermute | solution.py:40
  91.0 9.4 %collective-permute-start.6 = (f32[2,58,2,256]{3,2,1,0:T(2,128)S(1)}, f32[2,58,2,256]{3,2,1,0:T(2,128)S(1)}, u32[]{:S(2)}, u32[]{:S(2)}) collective-permute-start(f32[2,58,2,256]{3,2,1,0:T(2,128)S(1)} %get-tuple-element.104), channel_id=1, source_target_pairs={{0,1},{1,2},{2,3},{3,4},{4,5},{5,6},{6,7},{7,8},{8,9},{9,10},{10,1... | collective-permute-start | bytes 712712 | tf_op jit(solution)/shard_map/ppermute | solution.py:39
  93.0 8.4 %collective-permute-start.7 = (f32[2,58,2,256]{3,2,1,0:T(2,128)S(1)}, f32[2,58,2,256]{3,2,1,0:T(2,128)S(1)}, u32[]{:S(2)}, u32[]{:S(2)}) collective-permute-start(f32[2,58,2,256]{3,2,1,0:T(2,128)S(1)} %get-tuple-element.103), channel_id=1, source_target_pairs={{1,0},{2,1},{3,2},{4,3},{5,4},{6,5},{7,6},{8,7},{9,8},{10,9},{11,1... | collective-permute-start | bytes 712712 | tf_op jit(solution)/shard_map/ppermute | solution.py:40
  172.0 32.9 %all-to-all-start.1 = ((f32[64,6,116]{2,1,0:T(8,128)}), f32[64,6,116]{2,1,0:T(8,128)S(1)}, u32[]{:S(2)}, u32[]{:S(2)}) async-start(f32[64,6,116]{2,1,0:T(8,128)} %reshape.90), calls=%async_computation.1 | async-start | bytes 524288 | tf_op jit(solution)/shard_map/all_to_all | solution.py:128
Sparse Core Ops, SparseCore 0:
  105.6 62.4 all-gather.2
where the time goes:
time: 214 us; the launch traced here: 213 us
  waiting for transfers between devices  86.9 us (41%)
  starting transfers between devices  75.5 us (35%)
  other arithmetic  21.6 us (10%)
  between operations  14.7 us (7%)
  local copies, waits for them, and re-layouts  14.1 us (7%)
    all_gather x1, waiting for transfers between devices, over_pieces(): return lax.all_gather(x, axis).sum(0)  62.7 us
    ppermute x4, starting transfers between devices, padded(): after = lax.ppermute(leading, axis, down)  29.6 us
    all_to_all x1, starting transfers between devices, on_device(): lax.all_to_all(back_rows.reshape(col_count, capacity, 2 * levels), 'col',...  19.8 us
    all_to_all x1, starting transfers between devices, sent_together(): lax.all_to_all(both, axis, split_axis=split_dim, concat_axis=concat_dim,...  18.3 us
    all_to_all x1, waiting for transfers between devices, on_device(): lax.all_to_all(back_rows.reshape(col_count, capacity, 2 * levels), 'col',...  13.1 us
    ppermute x4, waiting for transfers between devices, padded(): before = lax.ppermute(last, axis, up)  8.43 us
    ppermute x4, starting transfers between devices, padded(): before = lax.ppermute(last, axis, up)  7.68 us
    add x8, other arithmetic, advance(): centre + courant_here * ((western - eastern) * 0.5)  7.12 us
  transfers between devices with their start and end apart: 11, of which 8 were waited for; matrix products, arithmetic and copies ran while one was open for 3% of the time, Pallas kernels for 0%

commit v1 on v0

--- a/solution.py
+++ b/solution.py
@@ -29,21 +29,9 @@
     )
 
 
-def padded(x, sides, width):
-    for axis, dim in sides:
-        peers, length = (lax.axis_size(axis), x.shape[dim])
-        up = [(i, (i + 1) % peers) for i in range(peers)]
-        down = [(j, i) for i, j in up]
-        last = lax.slice_in_dim(x, length - width, length, axis=dim)
-        leading = lax.slice_in_dim(x, 0, width, axis=dim)
-        before = lax.ppermute(last, axis, up)
-        after = lax.ppermute(leading, axis, down)
-        x = jnp.concatenate([before, x, after], axis=dim)
-    return x
-
-
-def over_pieces(x, axis):
-    return lax.all_gather(x, axis).sum(0)
+def shifted(x, by):
+    peers = lax.axis_size("grp")
+    return lax.ppermute(x, "grp", [(i, (i + by) % peers) for i in range(peers)])
 
 
 def condense(fields, cloudy):
@@ -112,28 +100,39 @@
     forcing = (phys_prof.reshape(columns, 2, levels).transpose(1, 2, 0) / STEPS)[:, :, None, :]
     courant_here = phys_cour.T[None, :, None, :]
     cloudy = cloud_flags.astype(jnp.float32)
-    crm_now = crm_state
-    for repeat in range(STEPS // 2):
-        widened = padded(crm_now, (("grp", 2),), 2)
-        middle = advance(widened, courant_here, forcing, cloudy)
-        crm_now = advance(middle, courant_here, forcing, cloudy)
-    cells_all = crm_state.shape[2] * lax.axis_size("grp")
+    left_one = shifted(crm_state, 1)
+    right_one = shifted(crm_state, -1)
+    left_two = shifted(left_one, 1)
+    right_two = shifted(right_one, -1)
+    crm_now = jnp.concatenate([left_two, left_one, crm_state, right_one, right_two], axis=2)
+    for repeat in range(STEPS):
+        crm_now = advance(crm_now, courant_here, forcing, cloudy)
+    pieces = lax.axis_size("grp")
+    cells_all = crm_state.shape[2] * pieces
     partial_value = jnp.sum(crm_now, axis=2) - jnp.sum(crm_state, axis=2)
-    totals = over_pieces(partial_value, "grp")
+    share = -(-levels // pieces)
+    spread = jnp.pad(partial_value, ((0, 0), (0, share * pieces - levels), (0, 0)))
+    spread = spread.reshape(2, pieces, share, columns).transpose(1, 0, 2, 3)
+    spread = spread.reshape(pieces, 2 * share, columns)
+    totals = lax.all_to_all(spread, "grp", split_axis=0, concat_axis=0, tiled=True).sum(0)
     increment = totals / cells_all
-    phys_inc = increment.transpose(2, 0, 1).reshape(columns, 2 * levels)
+    width = 2 * share
     back_rows = (
-        jnp.zeros((col_count * capacity, 2 * levels), jnp.float32).at[take_rows].set(phys_inc)
+        jnp.zeros((col_count * capacity, width), jnp.float32).at[take_rows].set(increment.T)
     )
     got_back = lax.all_to_all(
-        back_rows.reshape(col_count, capacity, 2 * levels),
+        back_rows.reshape(col_count, 1, capacity * width),
         "col",
         split_axis=0,
         concat_axis=0,
         tiled=True,
     )
-    tendency = got_back.reshape(col_count * capacity, 2 * levels)[sent_slot]
-    return (tendency, crm_now)
+    my_share = got_back.reshape(col_count * capacity, width)[sent_slot].T
+    copies = jnp.broadcast_to(my_share[None], (pieces, width, columns))
+    every = lax.all_to_all(copies, "grp", split_axis=0, concat_axis=0, tiled=True)
+    every = every.reshape(pieces, 2, share, columns).transpose(3, 1, 0, 2)
+    tendency = every.reshape(columns, 2, pieces * share)[:, :, :levels]
+    return (tendency.reshape(columns, 2 * levels), crm_now)
 
 
 def solution(mesh):

time: 214 us -> 149 us (0.70)
  waiting for transfers between devices: 86.9 us -> 15.7 us
  blocking collectives: 0 us -> 34.6 us
  starting transfers between devices: 75.5 us -> 52.5 us
  between operations: 14.7 us -> 1.39 us
  local copies, waits for them, and re-layouts: 14.1 us -> 18.8 us
    all_gather x1 -> x0, waiting for transfers between devices: 62.7 us -> none  [over_pieces(): return lax.all_gather(x, axis).sum(0)]
    all_to_all x0 -> x2, blocking collectives: none -> 34.6 us  [the longest x1 19.5 us: on_device(): lax.all_to_all(spread, 'grp', split_axis=0, concat_axis=0, tiled=True)]
    ppermute x8 -> x4, starting transfers between devices: 37.3 us -> 27.5 us  [shifted(): return lax.ppermute(x, 'grp', [(i, (i + by) % peers) for i in range(peers)])]
    ppermute x8 -> x4, waiting for transfers between devices: 11.2 us -> 1.66 us  [shifted(): return lax.ppermute(x, 'grp', [(i, (i + by) % peers) for i in range(peers)])]
    all_to_all x1, starting transfers between devices: 18.3 us -> 11.1 us  [sent_together(): lax.all_to_all(both, axis, split_axis=split_dim, concat_axis=concat_dim,...]
    concatenate x0 -> x1, local copies, waits for them, and re-layouts: none -> 6.39 us  [on_device(): jnp.concatenate([left_two, left_one, crm_state, right_one, right_two], ax...]
    all_to_all x1, starting transfers between devices: 19.8 us -> 13.9 us  [on_device(): lax.all_to_all(back_rows.reshape(col_count, 1, capacity * width), 'col',...]
    all_to_all x1, waiting for transfers between devices: 0.01 us -> 4.72 us  [sent_together(): lax.all_to_all(both, axis, split_axis=split_dim, concat_axis=concat_dim,...]
  transfers between devices with their start and end apart: 11 -> 6, of which waited for: 8 -> 4; matrix products, arithmetic and copies ran while one was open for 3% -> 10% of each run, Pallas kernels for 0% -> 0%
where the time goes in v1:
time: 149 us; the launch traced here: 147 us
  starting transfers between devices  52.5 us (35%)
  blocking collectives  34.6 us (23%)
  other arithmetic  23.2 us (16%)
  local copies, waits for them, and re-layouts  18.8 us (13%)
  waiting for transfers between devices  15.7 us (11%)
    ppermute x4, starting transfers between devices, shifted(): return lax.ppermute(x, 'grp', [(i, (i + by) % peers) for i in range(peers)])  27.5 us
    all_to_all x1, blocking collectives, on_device(): lax.all_to_all(spread, 'grp', split_axis=0, concat_axis=0, tiled=True)  19.5 us
    all_to_all x1, blocking collectives, on_device(): lax.all_to_all(copies, 'grp', split_axis=0, concat_axis=0, tiled=True)  15.1 us
    all_to_all x1, starting transfers between devices, on_device(): lax.all_to_all(back_rows.reshape(col_count, 1, capacity * width), 'col',...  13.9 us
    all_to_all x1, starting transfers between devices, sent_together(): lax.all_to_all(both, axis, split_axis=split_dim, concat_axis=concat_dim,...  11.1 us
    add x8, other arithmetic, advance(): centre + courant_here * ((western - eastern) * 0.5)  9.59 us
    all_to_all x1, waiting for transfers between devices, on_device(): lax.all_to_all(back_rows.reshape(col_count, 1, capacity * width), 'col',...  9.32 us
    concatenate x1, local copies, waits for them, and re-layouts, on_device(): jnp.concatenate([left_two, left_one, crm_state, right_one, right_two], ax...  6.39 us
  transfers between devices with their start and end apart: 6, of which 4 were waited for; matrix products, arithmetic and copies ran while one was open for 10% of the time, Pallas kernels for 0%

profile of v1, /device:TPU:1, one launch (start us, length us, event | category | flops | bytes accessed | tf_op | source)
XLA Modules:
  0.0 146.7 jit_solution(123523043484527233)
XLA Ops:
  0.6 5.0 %collective-permute-start = (f32[2,58,4,256]{3,2,1,0:T(4,128)}, f32[2,58,4,256]{3,2,1,0:T(4,128)S(1)}, u32[]{:S(2)}, u32[]{:S(2)}) collective-permute-start(f32[2,58,4,256]{3,2,1,0:T(4,128)} %param.11), channel_id=1, source_target_pairs={{0,1},{1,2},{2,3},{3,4},{4,5},{5,6},{6,7},{7,8},{8,9},{9,10},{10,1... | collective-permute-start | bytes 1425416 | tf_op jit(solution)/shard_map/ppermute | solution.py:34
  5.6 15.9 %collective-permute-start.2 = (f32[2,58,4,256]{3,2,1,0:T(4,128)}, f32[2,58,4,256]{3,2,1,0:T(4,128)S(1)}, u32[]{:S(2)}, u32[]{:S(2)}) collective-permute-start(f32[2,58,4,256]{3,2,1,0:T(4,128)} %param.11), channel_id=1, source_target_pairs={{0,15},{1,0},{2,1},{3,2},{4,3},{5,4},{6,5},{7,6},{8,7},{9,8},{10,9... | collective-permute-start | bytes 1425416 | tf_op jit(solution)/shard_map/ppermute | solution.py:34
  21.5 0.8 and_select_fusion
  22.4 0.8 compare_select_fusion.1
  23.2 1.4 scatter_custom_fusion
  24.6 1.0 copy.108
  25.7 1.1 gather_fusion
  27.0 1.1 gather_fusion.1
  28.2 1.0 pad_maximum_fusion.6
  29.2 11.1 %all-to-all-start = ((f32[64,6,174]{2,1,0:T(8,128)}), f32[64,6,174]{2,1,0:T(8,128)S(1)}, u32[]{:S(2)}, u32[]{:S(2)}) async-start(f32[64,6,174]{2,1,0:T(8,128)} %pad_maximum_fusion.6), calls=%async_computation | async-start | bytes 1048576 | tf_op jit(solution)/shard_map/all_to_all | solution.py:25
  40.3 0.6 reduce-window.6
  41.6 3.9 %while.11 = (s32[]{:T(128)}, s32[256]{0:T(256)S(1)}, s32[16,1024]{1,0:T(8,128)S(1)}, s32[16,1024]{1,0:T(8,128)S(1)}, s32[]{:T(128)}, /*index=5*/s32[]{:T(128)}) while((s32[]{:T(128)}, s32[256]{0:T(256)S(1)}, s32[16,1024]{1,0:T(8,128)S(1)}, s32[16,1024]{1,0:T(8,128)S(1)}, s32[]{:T(128)}, /*index=5*/s32[]{:T(128)}) %tuple.48), condition=%wide.region_4.5_spmd.clone, body=%wide.region_2.4_spmd.clone.sunk | while | flops 786691 | bytes 28755 | solution.py:95
  45.5 1.9 %collective-permute-start.1 = (f32[2,58,4,256]{3,2,1,0:T(4,128)S(1)}, f32[2,58,4,256]{3,2,1,0:T(4,128)}, u32[]{:S(2)}, u32[]{:S(2)}) collective-permute-start(f32[2,58,4,256]{3,2,1,0:T(4,128)S(1)} %collective-permute-done), channel_id=1, source_target_pairs={{0,1},{1,2},{2,3},{3,4},{4,5},{5,6},{6,7},{7,8},{8,9},{9,10},{10,1... | collective-permute-start | bytes 1425416 | tf_op jit(solution)/shard_map/ppermute | solution.py:34
  47.5 4.8 %collective-permute-start.3 = (f32[2,58,4,256]{3,2,1,0:T(4,128)S(1)}, f32[2,58,4,256]{3,2,1,0:T(4,128)}, u32[]{:S(2)}, u32[]{:S(2)}) collective-permute-start(f32[2,58,4,256]{3,2,1,0:T(4,128)S(1)} %collective-permute-done.2), channel_id=1, source_target_pairs={{0,15},{1,0},{2,1},{3,2},{4,3},{5,4},{6,5},{7,6},{8,7},{9,8},{10,9... | collective-permute-start | bytes 1425416 | tf_op jit(solution)/shard_map/ppermute | solution.py:34
  52.3 0.9 reduce_sum.47
  53.2 4.7 %all-to-all-done = f32[64,6,174]{2,1,0:T(8,128)S(1)} async-done(((f32[64,6,174]{2,1,0:T(8,128)}), f32[64,6,174]{2,1,0:T(8,128)S(1)}, u32[]{:S(2)}, u32[]{:S(2)}) %all-to-all-start) | async-done | bytes 267296 | tf_op jit(solution)/shard_map/all_to_all | solution.py:25
  58.0 0.7 gather_fusion.3
  59.0 0.7 gather_fusion.2
  59.9 0.8 collective-permute-done.1
  60.7 0.8 collective-permute-done.3
  61.5 6.4 %concatenate.60 = f32[2,58,20,256]{3,2,1,0:T(8,128)S(1)} concatenate(f32[2,58,4,256]{3,2,1,0:T(4,128)} %collective-permute-done.1, f32[2,58,4,256]{3,2,1,0:T(4,128)} %copy-done.2, f32[2,58,4,256]{3,2,1,0:T(4,128)S(1)} %copy-done, f32[2,58,4,256]{3,2,1,0:T(4,128)} %copy-done.3, f32[2,58,4,256]{3,2,1,0:T(4,128)} %collective-permute-done.3), dimensions={2} | concatenate | bytes 4751360 | tf_op jit(solution)/shard_map/concatenate | solution.py:107
  67.9 0.5 fusion.105
  68.5 1.9 %fusion.5 = f32[2,58,18,256]{3,2,1,0:T(8,128)S(1)} fusion(f32[2,1,18,256]{3,2,1,0:T(8,128)S(1)} %get-tuple-element.64, f32[2,57,18,256]{3,2,1,0:T(8,128)S(1)} %get-tuple-element.66, f32[2,57,18,256]{3,2,1,0:T(8,128)S(1)} %get-tuple-element.65, f32[2,1,18,256]{3,2,1,0:T(8,128)S(1)} %get-tuple-element.63, f32[2,58,20,256]{3,2,1,0:T(8,128)S(1)} %concatenate.60, ...), kind=kLoop, calls=%fused_computation.77 | loop fusion | flops 8017920 | bytes 13006848 | tf_op jit(solution)/shard_map/add | solution.py:52
  70.4 0.5 multiply_add_fusion
  70.9 0.3 fusion.41
  71.3 1.5 %fusion.37 = f32[2,58,16,256]{3,2,1,0:T(8,128)S(1)} fusion(f32[1,58,18,256]{3,2,1,0:T(8,128)S(1)} %get-tuple-element.60, f32[1,58,18,256]{3,2,1,0:T(8,128)S(1)} %get-tuple-element.59, f32[2,1,16,256]{3,2,1,0:T(8,128)S(1)} %get-tuple-element.62, f32[2,57,16,256]{3,2,1,0:T(8,128)S(1)} %fusion.41, f32[2,1,16,256]{3,2,1,0:T(8,128)S(1)} %get-tuple-element.61, ...), kind=kLoop, calls=%fused_computation.113 | loop fusion | flops 9027584 | bytes 6150144 | tf_op jit(solution)/shard_map/add | solution.py:52
  72.8 0.4 multiply_add_fusion.4
  73.4 1.4 fusion.32
  74.9 0.4 multiply_add_fusion.3
  75.3 0.3 fusion.39
  75.6 1.5 %fusion.27 = f32[2,58,12,256]{3,2,1,0:T(8,128)S(1)} fusion(f32[1,58,14,256]{3,2,1,0:T(8,128)S(1)} %get-tuple-element.72, f32[1,58,14,256]{3,2,1,0:T(8,128)S(1)} %get-tuple-element.71, f32[2,1,12,256]{3,2,1,0:T(8,128)S(1)} %get-tuple-element.80, f32[2,57,12,256]{3,2,1,0:T(8,128)S(1)} %fusion.39, f32[2,1,12,256]{3,2,1,0:T(8,128)S(1)} %get-tuple-element.79, ...), kind=kLoop, calls=%fused_computation.101 | loop fusion | flops 6770688 | bytes 4716544 | tf_op jit(solution)/shard_map/add | solution.py:52
  77.1 0.4 multiply_add_fusion.2
  77.8 1.5 %fusion.22 = f32[2,58,10,256]{3,2,1,0:T(8,128)S(1)} fusion(f32[1,58,12,256]{3,2,1,0:T(8,128)S(1)} %get-tuple-element.70, f32[1,58,12,256]{3,2,1,0:T(8,128)S(1)} %get-tuple-element.69, f32[2,1,10,256]{3,2,1,0:T(8,128)S(1)} %get-tuple-element.78, f32[2,57,10,256]{3,2,1,0:T(8,128)S(1)} %fusion.38, f32[2,1,10,256]{3,2,1,0:T(8,128)S(1)} %get-tuple-element.77, ...), kind=kLoop, calls=%fused_computation.95 | loop fusion | flops 5642240 | bytes 3999744 | tf_op jit(solution)/shard_map/add | solution.py:52
  79.3 0.4 multiply_add_fusion.1
  79.8 0.6 fusion.58
  80.7 0.6 fusion.53
  81.6 0.6 fusion.72
  82.5 0.9 fusion.103
  83.7 19.5 %all_to_all.20 = f32[16,8,256]{2,1,0:T(8,128)S(1)} all-to-all(f32[16,8,256]{2,1,0:T(8,128)S(1)} %copy.121), channel_id=1, replica_groups=mesh['col'=64,'grp'=16] {'grp'}, dimensions={0} | all-to-all | bytes 262144 | tf_op jit(solution)/shard_map/all_to_all | solution.py:117
  103.4 1.2 scatter_custom_fusion.1
  104.6 0.7 reshape.92
  105.3 13.9 %all-to-all-start.2 = ((f32[64,1,48]{2,1,0:T(1,128)}), f32[64,1,48]{2,1,0:T(1,128)S(1)}, u32[]{:S(2)}, u32[]{:S(2)}) async-start(f32[64,1,48]{2,1,0:T(1,128)} %bitcast.7), calls=%async_computation.2 | async-start | bytes 65536 | tf_op jit(solution)/shard_map/all_to_all | solution.py:123
  119.2 9.3 %all-to-all-done.2 = f32[64,1,48]{2,1,0:T(1,128)S(1)} async-done(((f32[64,1,48]{2,1,0:T(1,128)}), f32[64,1,48]{2,1,0:T(1,128)S(1)}, u32[]{:S(2)}, u32[]{:S(2)}) %all-to-all-start.2) | async-done | bytes 12320 | tf_op jit(solution)/shard_map/all_to_all | solution.py:123
  128.6 0.5 broadcast.397
  129.1 0.7 reduce.5
  129.9 0.7 gather_fusion.4
  130.7 15.1 %all_to_all.21 = f32[16,8,256]{2,1,0:T(8,128)S(1)} all-to-all(f32[16,8,256]{2,1,0:T(8,128)S(1)} %broadcast_in_dim.36), channel_id=1, replica_groups=mesh['col'=64,'grp'=16] {'grp'}, dimensions={0} | all-to-all | bytes 262144 | tf_op jit(solution)/shard_map/all_to_all | solution.py:132
  146.0 0.7 reshape.96
  (130 shorter events, 7.2 us)
Async XLA Ops:
  0.6 26.2 %copy-start.5 = (f32[256,58]{0,1:T(8,128)S(1)}, f32[256,58]{0,1:T(8,128)}, u32[]{:S(2)}) copy-start(f32[256,58]{0,1:T(8,128)} %param.8) | copy-start | bytes 178180
  0.6 44.9 %collective-permute-start = (f32[2,58,4,256]{3,2,1,0:T(4,128)}, f32[2,58,4,256]{3,2,1,0:T(4,128)S(1)}, u32[]{:S(2)}, u32[]{:S(2)}) collective-permute-start(f32[2,58,4,256]{3,2,1,0:T(4,128)} %param.11), channel_id=1, source_target_pairs={{0,1},{1,2},{2,3},{3,4},{4,5},{5,6},{6,7},{7,8},{8,9},{9,10},{10,1... | collective-permute-start | bytes 1425416 | tf_op jit(solution)/shard_map/ppermute | solution.py:34
  5.6 41.9 %collective-permute-start.2 = (f32[2,58,4,256]{3,2,1,0:T(4,128)}, f32[2,58,4,256]{3,2,1,0:T(4,128)S(1)}, u32[]{:S(2)}, u32[]{:S(2)}) collective-permute-start(f32[2,58,4,256]{3,2,1,0:T(4,128)} %param.11), channel_id=1, source_target_pairs={{0,15},{1,0},{2,1},{3,2},{4,3},{5,4},{6,5},{7,6},{8,7},{9,8},{10,9... | collective-permute-start | bytes 1425416 | tf_op jit(solution)/shard_map/ppermute | solution.py:34
  27.0 13.3 %copy-start.4 = (s32[16384]{0:T(1024)S(1)}, s32[16384]{0:T(1024)}, u32[]{:S(2)}) copy-start(s32[16384]{0:T(1024)} %param.9) | copy-start | bytes 196612
  28.1 17.4 %copy-start.6 = (s32[256]{0:T(256)S(1)}, s32[256]{0:T(256)}, u32[]{:S(2)}) copy-start(s32[256]{0:T(256)} %param.10) | copy-start | bytes 3076
  28.2 24.1 %copy-start = (f32[2,58,4,256]{3,2,1,0:T(4,128)S(1)}, f32[2,58,4,256]{3,2,1,0:T(4,128)}, u32[]{:S(2)}) copy-start(f32[2,58,4,256]{3,2,1,0:T(4,128)} %param.11) | copy-start | bytes 1425412
  29.2 28.8 %all-to-all-start = ((f32[64,6,174]{2,1,0:T(8,128)}), f32[64,6,174]{2,1,0:T(8,128)S(1)}, u32[]{:S(2)}, u32[]{:S(2)}) async-start(f32[64,6,174]{2,1,0:T(8,128)} %pad_maximum_fusion.6), calls=%async_computation | async-start | bytes 1048576 | tf_op jit(solution)/shard_map/all_to_all | solution.py:25
  45.5 13.5 %copy-start.2 = (f32[2,58,4,256]{3,2,1,0:T(4,128)}, f32[2,58,4,256]{3,2,1,0:T(4,128)S(1)}, u32[]{:S(2)}) copy-start(f32[2,58,4,256]{3,2,1,0:T(4,128)S(1)} %collective-permute-done) | copy-start | bytes 1425412
  45.5 15.2 %collective-permute-start.1 = (f32[2,58,4,256]{3,2,1,0:T(4,128)S(1)}, f32[2,58,4,256]{3,2,1,0:T(4,128)}, u32[]{:S(2)}, u32[]{:S(2)}) collective-permute-start(f32[2,58,4,256]{3,2,1,0:T(4,128)S(1)} %collective-permute-done), channel_id=1, source_target_pairs={{0,1},{1,2},{2,3},{3,4},{4,5},{5,6},{6,7},{7,8},{8,9},{9,10},{10,1... | collective-permute-start | bytes 1425416 | tf_op jit(solution)/shard_map/ppermute | solution.py:34
  47.5 13.2 %copy-start.3 = (f32[2,58,4,256]{3,2,1,0:T(4,128)}, f32[2,58,4,256]{3,2,1,0:T(4,128)S(1)}, u32[]{:S(2)}) copy-start(f32[2,58,4,256]{3,2,1,0:T(4,128)S(1)} %collective-permute-done.2) | copy-start | bytes 1425412
  47.5 14.1 %collective-permute-start.3 = (f32[2,58,4,256]{3,2,1,0:T(4,128)S(1)}, f32[2,58,4,256]{3,2,1,0:T(4,128)}, u32[]{:S(2)}, u32[]{:S(2)}) collective-permute-start(f32[2,58,4,256]{3,2,1,0:T(4,128)S(1)} %collective-permute-done.2), channel_id=1, source_target_pairs={{0,15},{1,0},{2,1},{3,2},{4,3},{5,4},{6,5},{7,6},{8,7},{9,8},{10,9... | collective-permute-start | bytes 1425416 | tf_op jit(solution)/shard_map/ppermute | solution.py:34
  81.6 1.8 %copy-start.1 = (f32[2,58,256]{2,1,0:T(8,128)S(1)}, f32[2,58,256]{2,1,0:T(8,128)}, u32[]{:S(2)}) copy-start(f32[2,58,256]{2,1,0:T(8,128)} %reduce_sum.47) | copy-start | bytes 356356
  105.3 23.2 %all-to-all-start.2 = ((f32[64,1,48]{2,1,0:T(1,128)}), f32[64,1,48]{2,1,0:T(1,128)S(1)}, u32[]{:S(2)}, u32[]{:S(2)}) async-start(f32[64,1,48]{2,1,0:T(1,128)} %bitcast.7), calls=%async_computation.2 | async-start | bytes 65536 | tf_op jit(solution)/shard_map/all_to_all | solution.py:123

commit v2 on v1

v2 whole, which is shorter than its diff:
```python
import jax
import jax.numpy as jnp
from jax import lax
from jax.experimental import pallas as pl
from jax.experimental.pallas import tpu as pltpu
from jax.sharding import PartitionSpec as P

STEPS = 8

diffuse_x = 0.25
diffuse_z = 0.2
sat_scale = 0.5
sat_slope = 0.3
cond_rate = 0.5
latent_gain = 0.4

LANES = 128
LEVELS = 58
GROWTH = sat_slope * 1.4426950408889634
VMEM = pl.BlockSpec(memory_space=pltpu.VMEM)
SMEM = pl.BlockSpec(memory_space=pltpu.SMEM)


def thirds(x):
    first = x.astype(jnp.bfloat16)
    rest = x - first.astype(jnp.float32)
    second = rest.astype(jnp.bfloat16)
    third = (rest - second.astype(jnp.float32)).astype(jnp.bfloat16)
    return first, second, third


def dot(a, b, dims=((1,), (0,))):
    return lax.dot_general(a, b, (dims, ((), ())), preferred_element_type=jnp.float32)


def earlier(hits, count):
    row = lax.broadcasted_iota(jnp.int32, (count, count), 0)
    col = lax.broadcasted_iota(jnp.int32, (count, count), 1)
    strict = jnp.where(row < col, 1.0, 0.0).astype(jnp.bfloat16)
    return dot(jnp.where(hits, 1.0, 0.0).astype(jnp.bfloat16), strict)


def rows_of(owners, count):
    left = owners[pl.ds(0, count, stride=2), :]
    right = owners[pl.ds(1, count, stride=2), :]
    return jnp.concatenate([left, right], axis=1)


def pack_kernel(me, owners, prof, cour, packed, picks):
    feats, columns = prof.shape
    levels = cour.shape[0]
    peers = owners.shape[0] * LANES // columns
    slots = picks.shape[0] // peers
    tiles = packed.shape[0] // peers
    half = LANES // 2
    mine = [owners[pl.ds(2 * me[0] + i, 1), :] for i in range(2)]
    target = jnp.concatenate(mine, axis=1) // columns
    hits = lax.broadcasted_iota(jnp.int32, (peers, columns), 0) == target
    order = earlier(hits, columns)
    chosen = jnp.concatenate(
        [jnp.where(hits & (order == k), 1.0, 0.0) for k in range(slots)], axis=0
    ).astype(jnp.bfloat16)
    picks[...] = chosen
    gap = jnp.zeros((half - levels, columns), jnp.float32)
    wind = jnp.concatenate([cour[...], gap], axis=0)
    blank = jnp.zeros_like(wind)
    table = jnp.concatenate(
        [prof[...], jnp.zeros((LANES - feats, columns), jnp.float32), wind, blank, blank, wind],
        axis=0,
    )
    rows = sum(dot(chosen, piece, ((1,), (1,))) for piece in thirds(table))
    for k in range(slots):
        packed[pl.ds(k, peers, stride=tiles), :] = rows[k * peers : (k + 1) * peers, :LANES]
    for j in range(slots // 2):
        low = rows[2 * j * peers : (2 * j + 1) * peers, LANES : 2 * LANES]
        high = rows[(2 * j + 1) * peers : (2 * j + 2) * peers, 2 * LANES :]
        packed[pl.ds(slots + j, peers, stride=tiles), :] = low + high


def landing_kernel(me, owners, lands):
    columns = lands.shape[1]
    peers = owners.shape[0] * LANES // columns
    slots = lands.shape[0] // peers
    own = rows_of(owners, peers)
    hits = own // columns == me[0]
    order = earlier(hits, columns)
    local = (own % columns + 1).astype(jnp.float32)
    place = lax.broadcasted_iota(jnp.int32, (peers, columns), 1).astype(jnp.float32)
    for k in range(slots):
        spot = jnp.sum(jnp.where(hits & (order == k), local, 0.0), axis=1, keepdims=True)
        lands[k * peers : (k + 1) * peers, :] = jnp.where(spot - 1.0 == place, 1.0, 0.0).astype(
            jnp.bfloat16
        )


def forcing_kernel(got, lands, flags, force, east, west, rate):
    columns = lands.shape[1]
    fields, lane_tiles, tall, _ = force.shape
    slots = 6
    peers = lands.shape[0] // slots
    tiles = got.shape[0] // peers
    half = LANES // 2
    landed = lands[...]
    stacked = jnp.concatenate(
        [got[pl.ds(k, peers, stride=tiles), :] for k in range(slots)], axis=0
    )
    forcing = sum(dot(piece, landed) for piece in thirds(stacked.T)) / STEPS
    wind = jnp.zeros((half, columns), jnp.float32)
    for j in range(slots // 2):
        turned = thirds(got[pl.ds(slots + j, peers, stride=tiles), :].T)
        for odd in range(2):
            where_to = landed[(2 * j + odd) * peers : (2 * j + odd + 1) * peers]
            for piece in turned:
                wind = wind + dot(piece[odd * half : (odd + 1) * half], where_to)
    fraction = cond_rate * flags[...].astype(jnp.float32)
    fraction = jnp.broadcast_to(fraction, (8, columns))
    for c in range(lane_tiles):
        lanes = slice(c * LANES, (c + 1) * LANES)
        east[c] = diffuse_x - 0.5 * wind[:tall, lanes]
        west[c] = diffuse_x + 0.5 * wind[:tall, lanes]
        rate[0, c] = fraction[:, lanes]
        rate[1, c] = (latent_gain * GROWTH) * fraction[:, lanes]
        for f in range(fields):
            rows = forcing[f * LEVELS : (f + 1) * LEVELS, lanes]
            force[f, c, :LEVELS, :] = rows * GROWTH if f == 0 else rows


BLOCKS = ((1, 9, 11), (2, 10), (3, 9), (4, 8), (5, 7), (6,), (6,), (8,))
GROUPS = (2, 2, 2, 2, 2, 4, 4, 4)


def steps_kernel(
    force, east, west, rate, own, left1, right1, left2, right2, final, change, even, odd, sums
):
    fields, levels, lane_tiles, _, _ = even.shape
    slabs = (left2, left1, own, right1, right2)
    cells = 8 // lane_tiles
    share = change.shape[1] // fields
    sums[...] = jnp.zeros_like(sums)

    def place(z, carry):
        for f in range(fields):
            for c in range(lane_tiles):
                for s, slab in enumerate(slabs):
                    value = slab[f * levels + z, c * cells : (c + 1) * cells, :]
                    value = GROWTH * value - 1.0 if f == 0 else value + sat_scale
                    even[f, z, c, s * cells : (s + 1) * cells, :] = value
        return carry

    lax.fori_loop(0, levels, place, 0)
    rates = [[jnp.broadcast_to(rate[f, c, :1, :], (8, LANES)) for c in range(lane_tiles)] for f in range(2)]

    def at_level(step, source, z, below, above):
        results = []
        for c in range(lane_tiles):
            wide = [jnp.broadcast_to(w[c, pl.ds(z, 1), :], (8, LANES)) for w in (east, west)]
            push = [jnp.broadcast_to(force[f, c, pl.ds(z, 1), :], (8, LANES)) for f in range(fields)]
            for row in BLOCKS[step]:
                rows = slice(row, row + 8)
                stepped = []
                for f in range(fields):
                    stepped.append(
                        (1.0 - 2.0 * diffuse_x - 2.0 * diffuse_z) * source[f, z, c, rows, :]
                        + diffuse_z * (source[f, below, c, rows, :] + source[f, above, c, rows, :])
                        + (
                            wide[0] * source[f, z, c, row + 1 : row + 9, :]
                            + wide[1] * source[f, z, c, row - 1 : row + 7, :]
                        )
                        + push[f]
                    )
                energy, moisture = stepped
                excess = jnp.maximum(moisture - jnp.exp2(energy), 0.0)
                results.append((c, row, energy + rates[1][c] * excess, moisture - rates[0][c] * excess))
        return results

    def store(step, target, z, results):
        for c, row, energy, moisture in results:
            if step < STEPS - 1:
                target[0, z, c, row : row + 8, :] = energy
                target[1, z, c, row : row + 8, :] = moisture
                continue
            energy = (energy + 1.0) * (1.0 / GROWTH)
            moisture = moisture - sat_scale
            for f, now in enumerate((energy, moisture)):
                now = now[:cells]
                start = own[f * levels + z, c * cells : (c + 1) * cells, :]
                final[f * levels + z, c * cells : (c + 1) * cells, :] = now
                sums[f, c, pl.ds(z, 1), :] = jnp.sum(now - start, axis=0, keepdims=True)

    for step in range(STEPS):
        source, target = (even, odd) if step % 2 == 0 else (odd, even)
        many = GROUPS[step]

        def body(i, carry, step=step, source=source, target=target, many=many):
            zs = [i * many + k for k in range(many)]
            found = [
                at_level(step, source, z, jnp.maximum(z - 1, 0), jnp.minimum(z + 1, levels - 1))
                for z in zs
            ]
            for z, results in zip(zs, found):
                store(step, target, z, results)
            return carry

        lax.fori_loop(0, levels // many, body, 0)
        for z in range(levels // many * many, levels):
            store(step, target, z, at_level(step, source, z, max(z - 1, 0), min(z + 1, levels - 1)))
    for f in range(fields):
        for c in range(lane_tiles):
            for g in range(change.shape[0]):
                change[g, f * share : (f + 1) * share, c * LANES : (c + 1) * LANES] = sums[
                    f, c, g * share : (g + 1) * share, :
                ]


def return_kernel(inverse, parts, lands, sent):
    pieces, rows, columns = parts.shape
    peers = sent.shape[0]
    slots = lands.shape[0] // peers
    total = parts[0]
    for g in range(1, pieces):
        total = total + parts[g]
    total = total * inverse[0]
    many = jnp.concatenate([total] * (LANES // rows), axis=0)
    placed = sum(dot(lands[...], piece, ((1,), (1,))) for piece in thirds(many))
    lane = lax.broadcasted_iota(jnp.int32, (peers, LANES), 1) // rows
    out = jnp.zeros((peers, LANES), jnp.float32)
    for k in range(slots):
        out = out + jnp.where(lane == k, placed[k * peers : (k + 1) * peers], 0.0)
    sent[...] = out


def arrive_kernel(got, picks, copies):
    peers = got.shape[0]
    slots = picks.shape[0] // peers
    pieces, rows, columns = copies.shape
    turned = thirds(got[...].T)
    share = jnp.zeros((rows, columns), jnp.float32)
    for k in range(slots):
        where_to = picks[k * peers : (k + 1) * peers]
        for piece in turned:
            share = share + dot(piece, where_to)[k * rows : (k + 1) * rows]
    for g in range(pieces):
        copies[g] = share


def spread_kernel(every, tendency):
    pieces, rows, columns = every.shape
    share = rows // 2
    levels = tendency.shape[0] // 2
    for f in range(2):
        for g in range(pieces):
            here = min(share, levels - g * share)
            if here > 0:
                start = f * levels + g * share
                tendency[start : start + here, :] = every[g, f * share : f * share + here, :]


def call(kernel, outs, scratch=(), scalars=0, inputs=0):
    return pl.pallas_call(
        kernel,
        out_shape=outs,
        in_specs=[SMEM] * scalars + [VMEM] * inputs,
        out_specs=jax.tree.map(lambda _: VMEM, outs),
        scratch_shapes=list(scratch),
        compiler_params=pltpu.CompilerParams(vmem_limit_bytes=16 * 1024 * 1024),
    )


def shifted(x, by):
    peers = lax.axis_size("grp")
    return lax.ppermute(x, "grp", [(i, (i + by) % peers) for i in range(peers)])


def traded(x, axis):
    return lax.all_to_all(x, axis, split_axis=0, concat_axis=0, tiled=True)


def flat(x):
    f, z, cells, columns = x.shape
    x = x.reshape(f, z, cells, columns // LANES, LANES).transpose(0, 1, 3, 2, 4)
    return x.reshape(f * z, cells * columns // LANES, LANES)


def on_device(profiles, courant, owner_map, cloud_flags, crm_state):
    columns, feats = profiles.shape
    levels = courant.shape[1]
    col_count = lax.axis_size("col")
    pieces = lax.axis_size("grp")
    fields, _, cells, _ = crm_state.shape
    per_peer = columns // col_count
    capacity = per_peer + min(2, per_peer)
    share = -(-levels // pieces)
    tall = share * pieces
    lane_tiles = columns // LANES
    f32, bf16 = jnp.float32, jnp.bfloat16
    S = jax.ShapeDtypeStruct
    me = lax.axis_index("col").reshape(1)
    owners = owner_map.reshape(-1, LANES)
    left1, right1 = shifted(crm_state, 1), shifted(crm_state, -1)
    tiles = capacity + capacity // 2
    packed, picks = call(
        pack_kernel,
        (S((col_count * tiles, LANES), f32), S((capacity * col_count, columns), bf16)),
        (),
        1,
        3,
    )(me, owners, profiles.T, courant.T)
    got = traded(packed.reshape(col_count, 1, tiles * LANES), "col").reshape(packed.shape)
    lands = call(landing_kernel, S((capacity * col_count, columns), bf16), (), 1, 1)(me, owners)
    left2, right2 = shifted(left1, 1), shifted(right1, -1)
    forces = call(
        forcing_kernel,
        (
            S((fields, lane_tiles, tall, LANES), f32),
            S((lane_tiles, tall, LANES), f32),
            S((lane_tiles, tall, LANES), f32),
            S((2, lane_tiles, 8, LANES), f32),
        ),
        (),
        0,
        3,
    )(got, lands, cloud_flags.reshape(1, columns))
    slabs = [flat(x) for x in (crm_state, left1, right1, left2, right2)]
    rows, change = call(
        steps_kernel,
        (S(slabs[0].shape, f32), S((pieces, 2 * share, columns), f32)),
        [pltpu.VMEM((fields, levels, lane_tiles, 24, LANES), f32)] * 2
        + [pltpu.VMEM((fields, lane_tiles, tall, LANES), f32)],
        0,
        9,
    )(*forces, *slabs)
    rows = rows.reshape(fields, levels, lane_tiles, cells, LANES).transpose(0, 1, 3, 2, 4)
    crm_final = rows.reshape(crm_state.shape)
    parts = traded(change, "grp")
    inverse = jnp.full((1,), 1.0 / (pieces * cells), f32)
    back = call(return_kernel, S((col_count, LANES), f32), (), 1, 2)(inverse, parts, lands)
    back = traded(back.reshape(col_count, 1, LANES), "col").reshape(back.shape)
    copies = call(arrive_kernel, S((pieces, 2 * share, columns), f32), (), 0, 2)(back, picks)
    every = traded(copies, "grp")
    tendency = call(spread_kernel, S((feats, columns), f32), (), 0, 1)(every)
    return tendency.T, crm_final


def solution(mesh):
    placed = (P("col", None), P("col", None), P(), P("col"), P(None, None, "grp", "col"))
    return jax.shard_map(
        on_device,
        mesh=mesh,
        in_specs=placed,
        out_specs=(P("col", None), P(None, None, "grp", "col")),
        check_vma=False,
    )
```

time: 149 us -> 123 us (0.83)
  other arithmetic: 23.2 us -> 0 us
  blocking collectives: 34.6 us -> 52.8 us
  local copies, waits for them, and re-layouts: 18.8 us -> 2.59 us
  Pallas kernels: 0 us -> 14.5 us
  starting transfers between devices: 52.5 us -> 38.8 us
  waiting for transfers between devices: 15.7 us -> 12.1 us
    all_to_all x2 -> x3, blocking collectives: 34.6 us -> 52.8 us  [traded(): return lax.all_to_all(x, axis, split_axis=0, concat_axis=0, tiled=True)]
    pallas_call x0 -> x7, Pallas kernels: none -> 14.5 us  [the longest x1 10.9 us: on_device(): call(steps_kernel, (S(slabs[0].shape, f32), S((pieces, 2 * share, columns...]
    all_to_all x2 -> x1, starting transfers between devices: 25 us -> 11.2 us  [traded(): return lax.all_to_all(x, axis, split_axis=0, concat_axis=0, tiled=True)]
    add x33 -> x0, other arithmetic: 12.5 us -> none  [the longest x8 9.59 us: advance(): centre + courant_here * ((western - eastern) * 0.5)]
    all_to_all x2 -> x1, waiting for transfers between devices: 14 us -> 6.42 us  [traded(): return lax.all_to_all(x, axis, split_axis=0, concat_axis=0, tiled=True)]
    concatenate x3 -> x0, local copies, waits for them, and re-layouts: 6.41 us -> none  [the longest x1 6.39 us: on_device(): jnp.concatenate([left_two, left_one, crm_state, right_one, right_two], ax...]
    reduce_sum x20 -> x0, other arithmetic: 5.08 us -> none  [the longest x16 3.01 us: match_block(): return (found + jnp.sum(jnp.where(hits, anchors[None, :], 0), axis=1), None)]
    gather x6 -> x0, local copies, waits for them, and re-layouts: 4.55 us -> none  [the longest x1 1.12 us: on_device(): padded_prof[send_rows].reshape(col_count, capacity, profiles.shape[1])]
  transfers between devices with their start and end apart: 6 -> 5, of which waited for: 4 -> 3; matrix products, arithmetic and copies ran while one was open for 10% -> 0% of each run, Pallas kernels for 0% -> 2%
where the time goes in v2:
time: 123 us; the launch traced here: 122 us
  blocking collectives  52.8 us (43%)
  starting transfers between devices  38.8 us (32%)
  Pallas kernels  14.5 us (12%)
  waiting for transfers between devices  12.1 us (10%)
  local copies, waits for them, and re-layouts  2.59 us (2%)
    all_to_all x3, blocking collectives, traded(): return lax.all_to_all(x, axis, split_axis=0, concat_axis=0, tiled=True)  52.8 us
    ppermute x4, starting transfers between devices, shifted(): return lax.ppermute(x, 'grp', [(i, (i + by) % peers) for i in range(peers)])  27.6 us
    all_to_all x1, starting transfers between devices, traded(): return lax.all_to_all(x, axis, split_axis=0, concat_axis=0, tiled=True)  11.2 us
    pallas_call x1, Pallas kernels, on_device(): call(steps_kernel, (S(slabs[0].shape, f32), S((pieces, 2 * share, columns...  10.9 us
    all_to_all x1, waiting for transfers between devices, traded(): return lax.all_to_all(x, axis, split_axis=0, concat_axis=0, tiled=True)  6.42 us
    ppermute x4, waiting for transfers between devices, shifted(): return lax.ppermute(x, 'grp', [(i, (i + by) % peers) for i in range(peers)])  5.66 us
    unnamed x12, local copies, waits for them, and re-layouts  2.59 us
  transfers between devices with their start and end apart: 5, of which 3 were waited for; matrix products, arithmetic and copies ran while one was open for 0% of the time, Pallas kernels for 2%

profile of v2, /device:TPU:1, one launch (start us, length us, event | category | flops | bytes accessed | tf_op | source)
XLA Modules:
  0.0 121.5 jit_solution(18090387211768497964)
XLA Ops:
  0.6 18.8 %collective-permute-start.1 = (f32[2,58,4,256]{3,2,1,0:T(4,128)}, f32[2,58,4,256]{3,2,1,0:T(4,128)S(1)}, u32[]{:S(2)}, u32[]{:S(2)}) collective-permute-start(f32[2,58,4,256]{3,2,1,0:T(4,128)} %param.9), channel_id=1, source_target_pairs={{0,15},{1,0},{2,1},{3,2},{4,3},{5,4},{6,5},{7,6},{8,7},{9,8},{10,9... | collective-permute-start | bytes 1425416 | tf_op jit(solution)/shard_map/ppermute | solution.py:271
  19.4 1.9 %collective-permute-start = (f32[2,58,4,256]{3,2,1,0:T(4,128)}, f32[2,58,4,256]{3,2,1,0:T(4,128)S(1)}, u32[]{:S(2)}, u32[]{:S(2)}) collective-permute-start(f32[2,58,4,256]{3,2,1,0:T(4,128)} %param.9), channel_id=1, source_target_pairs={{0,1},{1,2},{2,3},{3,4},{4,5},{5,6},{6,7},{7,8},{8,9},{9,10},{10,1... | collective-permute-start | bytes 1425416 | tf_op jit(solution)/shard_map/ppermute | solution.py:271
  21.3 0.0 copy-start.1
  21.3 0.8 copy-done.1
  22.2 0.0 copy-start.3
  22.2 0.9 copy-done.3
  23.1 0.0 copy-start.4
  23.1 0.8 copy-done.4
  23.9 1.3 %shard_map.68 = (f32[576,128]{1,0:T(8,128)}, bf16[384,256]{1,0:T(8,128)(2,1)S(1)}) custom-call(s32[1]{0:T(128)} %bitcast.me, s32[128,128]{1,0:T(8,128)S(1)} %bitcast.48, f32[116,256]{1,0:T(8,128)S(1)} %bitcast.52, f32[58,256]{1,0:T(8,128)S(1)} %bitcast.53), custom_call_target="tpu_custom_call" | custom-call | tf_op jit(solution)/shard_map/pallas_call | solution.py:301
  25.3 0.0 copy-start.2
  25.3 0.0 copy-start.5
  25.3 11.2 %all-to-all-start = ((f32[64,1,1152]{2,1,0:T(1,128)}), f32[64,1,1152]{2,1,0:T(1,128)S(1)}, u32[]{:S(2)}, u32[]{:S(2)}) async-start(f32[64,1,1152]{2,1,0:T(1,128)} %bitcast.4), calls=%async_computation | async-start | bytes 589824 | tf_op jit(solution)/shard_map/all_to_all | solution.py:275
  36.5 0.0 copy-start
  36.5 0.0 collective-permute-done.1
  36.5 5.0 %collective-permute-start.3 = (f32[2,58,4,256]{3,2,1,0:T(4,128)S(1)}, f32[2,58,4,256]{3,2,1,0:T(4,128)S(1)}, u32[]{:S(2)}, u32[]{:S(2)}) collective-permute-start(f32[2,58,4,256]{3,2,1,0:T(4,128)S(1)} %collective-permute-done.1), channel_id=1, source_target_pairs={{0,15},{1,0},{2,1},{3,2},{4,3},{5,4},{6,5},{7,6},{8,7},{9,8},{10,9... | collective-permute-start | bytes 1425416 | tf_op jit(solution)/shard_map/ppermute | solution.py:271
  41.5 0.0 collective-permute-done
  41.5 1.9 %collective-permute-start.2 = (f32[2,58,4,256]{3,2,1,0:T(4,128)S(1)}, f32[2,58,4,256]{3,2,1,0:T(4,128)S(1)}, u32[]{:S(2)}, u32[]{:S(2)}) collective-permute-start(f32[2,58,4,256]{3,2,1,0:T(4,128)S(1)} %collective-permute-done), channel_id=1, source_target_pairs={{0,1},{1,2},{2,3},{3,4},{4,5},{5,6},{6,7},{7,8},{8,9},{9,10},{10,1... | collective-permute-start | bytes 1425416 | tf_op jit(solution)/shard_map/ppermute | solution.py:271
  43.4 0.0 copy-done.2
  43.4 0.3 shard_map.69.lands
  43.7 6.4 %all-to-all-done = f32[64,1,1152]{2,1,0:T(1,128)S(1)} async-done(((f32[64,1,1152]{2,1,0:T(1,128)}), f32[64,1,1152]{2,1,0:T(1,128)S(1)}, u32[]{:S(2)}, u32[]{:S(2)}) %all-to-all-start) | async-done | bytes 294944 | tf_op jit(solution)/shard_map/all_to_all | solution.py:275
  50.2 0.0 copy-done.5
  50.2 0.5 shard_map.70
  50.6 0.6 collective-permute-done.3
  51.2 5.1 %collective-permute-done.2 = f32[2,58,4,256]{3,2,1,0:T(4,128)S(1)} collective-permute-done((f32[2,58,4,256]{3,2,1,0:T(4,128)S(1)}, f32[2,58,4,256]{3,2,1,0:T(4,128)S(1)}, u32[]{:S(2)}, u32[]{:S(2)}) %collective-permute-start.2) | collective-permute-done | bytes 475168 | tf_op jit(solution)/shard_map/ppermute | solution.py:271
  56.3 0.0 copy-done
  56.3 10.9 %shard_map.71 = (f32[116,8,128]{2,1,0:T(8,128)}, f32[16,8,256]{2,1,0:T(8,128)S(1)}) custom-call(f32[2,2,64,128]{3,2,1,0:T(8,128)S(1)} %get-tuple-element.11.force, f32[2,64,128]{2,1,0:T(8,128)S(1)} %get-tuple-element.12.east, f32[2,64,128]{2,1,0:T(8,128)S(1)} %get-tuple-element.13.west, f32[2,2,8,128]{3,2,1,0:T(8,128)S(1)} %get-tuple-element.14.rate, ...), custom_call_target="tpu_custom_call" | custom-call | tf_op jit(solution)/shard_map/pallas_call | solution.py:324
  67.2 14.6 %all_to_all.20.parts = f32[16,8,256]{2,1,0:T(8,128)S(1)} all-to-all(f32[16,8,256]{2,1,0:T(8,128)S(1)} %get-tuple-element.15), channel_id=1, replica_groups=mesh['col'=64,'grp'=16] {'grp'}, dimensions={0} | all-to-all | bytes 262144 | tf_op jit(solution)/shard_map/all_to_all | solution.py:275
  81.8 0.3 shard_map.72
  82.1 23.1 %all_to_all.21 = f32[64,1,128]{2,1,0:T(1,128)S(1)} all-to-all(f32[64,1,128]{2,1,0:T(1,128)S(1)} %bitcast.50), channel_id=1, replica_groups=mesh['col'=64,'grp'=16] {'col'}, dimensions={0} | all-to-all | bytes 65536 | tf_op jit(solution)/shard_map/all_to_all | solution.py:275
  105.2 0.5 shard_map.73
  105.7 15.1 %all_to_all.22.every = f32[16,8,256]{2,1,0:T(8,128)S(1)} all-to-all(f32[16,8,256]{2,1,0:T(8,128)S(1)} %shard_map.73), channel_id=1, replica_groups=mesh['col'=64,'grp'=16] {'grp'}, dimensions={0} | all-to-all | bytes 262144 | tf_op jit(solution)/shard_map/all_to_all | solution.py:275
  120.8 0.7 shard_map.74
Async XLA Ops:
  0.6 35.9 %collective-permute-start.1 = (f32[2,58,4,256]{3,2,1,0:T(4,128)}, f32[2,58,4,256]{3,2,1,0:T(4,128)S(1)}, u32[]{:S(2)}, u32[]{:S(2)}) collective-permute-start(f32[2,58,4,256]{3,2,1,0:T(4,128)} %param.9), channel_id=1, source_target_pairs={{0,15},{1,0},{2,1},{3,2},{4,3},{5,4},{6,5},{7,6},{8,7},{9,8},{10,9... | collective-permute-start | bytes 1425416 | tf_op jit(solution)/shard_map/ppermute | solution.py:271
  19.4 22.1 %collective-permute-start = (f32[2,58,4,256]{3,2,1,0:T(4,128)}, f32[2,58,4,256]{3,2,1,0:T(4,128)S(1)}, u32[]{:S(2)}, u32[]{:S(2)}) collective-permute-start(f32[2,58,4,256]{3,2,1,0:T(4,128)} %param.9), channel_id=1, source_target_pairs={{0,1},{1,2},{2,3},{3,4},{4,5},{5,6},{6,7},{7,8},{8,9},{9,10},{10,1... | collective-permute-start | bytes 1425416 | tf_op jit(solution)/shard_map/ppermute | solution.py:271
  21.3 0.8 copy-start.1
  22.2 0.9 copy-start.3
  23.1 0.8 copy-start.4
  25.3 18.2 %copy-start.2 = (s32[16384]{0:T(1024)S(1)}, s32[16384]{0:T(1024)}, u32[]{:S(2)}) copy-start(s32[16384]{0:T(1024)} %param.7) | copy-start | bytes 196612
  25.3 24.9 %copy-start.5 = (s32[256]{0:T(256)S(1)}, s32[256]{0:T(256)}, u32[]{:S(2)}) copy-start(s32[256]{0:T(256)} %param.8) | copy-start | bytes 3076
  25.3 24.9 %all-to-all-start = ((f32[64,1,1152]{2,1,0:T(1,128)}), f32[64,1,1152]{2,1,0:T(1,128)S(1)}, u32[]{:S(2)}, u32[]{:S(2)}) async-start(f32[64,1,1152]{2,1,0:T(1,128)} %bitcast.4), calls=%async_computation | async-start | bytes 589824 | tf_op jit(solution)/shard_map/all_to_all | solution.py:275
  36.5 19.8 %copy-start = (f32[2,58,4,256]{3,2,1,0:T(4,128)S(1)}, f32[2,58,4,256]{3,2,1,0:T(4,128)}, u32[]{:S(2)}) copy-start(f32[2,58,4,256]{3,2,1,0:T(4,128)} %param.9) | copy-start | bytes 1425412
  36.5 14.7 %collective-permute-start.3 = (f32[2,58,4,256]{3,2,1,0:T(4,128)S(1)}, f32[2,58,4,256]{3,2,1,0:T(4,128)S(1)}, u32[]{:S(2)}, u32[]{:S(2)}) collective-permute-start(f32[2,58,4,256]{3,2,1,0:T(4,128)S(1)} %collective-permute-done.1), channel_id=1, source_target_pairs={{0,15},{1,0},{2,1},{3,2},{4,3},{5,4},{6,5},{7,6},{8,7},{9,8},{10,9... | collective-permute-start | bytes 1425416 | tf_op jit(solution)/shard_map/ppermute | solution.py:271
  41.5 14.8 %collective-permute-start.2 = (f32[2,58,4,256]{3,2,1,0:T(4,128)S(1)}, f32[2,58,4,256]{3,2,1,0:T(4,128)S(1)}, u32[]{:S(2)}, u32[]{:S(2)}) collective-permute-start(f32[2,58,4,256]{3,2,1,0:T(4,128)S(1)} %collective-permute-done), channel_id=1, source_target_pairs={{0,1},{1,2},{2,3},{3,4},{4,5},{5,6},{6,7},{7,8},{8,9},{9,10},{10,1... | collective-permute-start | bytes 1425416 | tf_op jit(solution)/shard_map/ppermute | solution.py:271

commit v3 on v2

--- a/solution.py
+++ b/solution.py
@@ -1,3 +1,5 @@
+import functools
+
 import jax
 import jax.numpy as jnp
 from jax import lax
@@ -15,7 +17,6 @@
 latent_gain = 0.4
 
 LANES = 128
-LEVELS = 58
 GROWTH = sat_slope * 1.4426950408889634
 VMEM = pl.BlockSpec(memory_space=pltpu.VMEM)
 SMEM = pl.BlockSpec(memory_space=pltpu.SMEM)
@@ -93,12 +94,13 @@
         )
 
 
-def forcing_kernel(got, lands, flags, force, east, west, rate):
+def forcing_kernel(got, lands, flags, force, east, west, rate, rows):
     columns = lands.shape[1]
-    fields, lane_tiles, tall, _ = force.shape
-    slots = 6
-    peers = lands.shape[0] // slots
-    tiles = got.shape[0] // peers
+    tiles = 9
+    peers = got.shape[0] // tiles
+    slots = lands.shape[0] // peers
+    levels = east.shape[0]
+    lane_tiles = rows.shape[0]
     half = LANES // 2
     landed = lands[...]
     stacked = jnp.concatenate(
@@ -112,104 +114,209 @@
             where_to = landed[(2 * j + odd) * peers : (2 * j + odd + 1) * peers]
             for piece in turned:
                 wind = wind + dot(piece[odd * half : (odd + 1) * half], where_to)
-    fraction = cond_rate * flags[...].astype(jnp.float32)
-    fraction = jnp.broadcast_to(fraction, (8, columns))
     for c in range(lane_tiles):
         lanes = slice(c * LANES, (c + 1) * LANES)
-        east[c] = diffuse_x - 0.5 * wind[:tall, lanes]
-        west[c] = diffuse_x + 0.5 * wind[:tall, lanes]
-        rate[0, c] = fraction[:, lanes]
-        rate[1, c] = (latent_gain * GROWTH) * fraction[:, lanes]
-        for f in range(fields):
-            rows = forcing[f * LEVELS : (f + 1) * LEVELS, lanes]
-            force[f, c, :LEVELS, :] = rows * GROWTH if f == 0 else rows
-
-
-BLOCKS = ((1, 9, 11), (2, 10), (3, 9), (4, 8), (5, 7), (6,), (6,), (8,))
-GROUPS = (2, 2, 2, 2, 2, 4, 4, 4)
-
-
-def steps_kernel(
-    force, east, west, rate, own, left1, right1, left2, right2, final, change, even, odd, sums
-):
-    fields, levels, lane_tiles, _, _ = even.shape
-    slabs = (left2, left1, own, right1, right2)
-    cells = 8 // lane_tiles
-    share = change.shape[1] // fields
+        rows[c, :LANES, :] = forcing[:, lanes]
+        rows[c, LANES:, :] = 0.5 * wind[:, lanes]
+    even = lax.broadcasted_iota(jnp.int32, (8, LANES), 0) % 2 == 0
+
+    def woven(line):
+        first, second = (jnp.broadcast_to(rows[c, pl.ds(line, 1), :], (8, LANES)) for c in (0, 1))
+        return jnp.where(even, first, second)
+
+    def weave(z, carry):
+        force[z] = GROWTH * woven(z)
+        force[levels + z] = woven(levels + z)
+        along = woven(LANES + z)
+        east[z] = diffuse_x - along
+        west[z] = diffuse_x + along
+        return carry
+
+    lax.fori_loop(0, levels, weave, 0, unroll=2)
+    fraction = cond_rate * flags[...].astype(jnp.float32)
+    first, second = (
+        jnp.broadcast_to(fraction[:, c * LANES : (c + 1) * LANES], (8, LANES)) for c in (0, 1)
+    )
+    fraction = jnp.where(even, first, second)
+    rate[0] = (latent_gain * GROWTH) * fraction
+    rate[1] = fraction
+
+
+def place(slab, first, target, z):
+    levels = target.shape[0] // 2
+    for f in range(2):
+        for c in range(2):
+            value = slab[f * levels + z, 4 * c : 4 * c + 4, :]
+            value = GROWTH * value - 1.0 if f == 0 else value + sat_scale
+            target[f * levels + z, pl.ds(2 * first + c, 4, stride=2), :] = value
+
+
+def march(force, east, west, rates, source, z, below, above, starts):
+    levels = east.shape[0]
+    results = []
+    for row in starts:
+        stepped = []
+        for f in range(2):
+            base = f * levels
+            stepped.append(
+                (1.0 - 2.0 * diffuse_x - 2.0 * diffuse_z) * source[base + z, row : row + 8, :]
+                + diffuse_z
+                * (source[base + below, row : row + 8, :] + source[base + above, row : row + 8, :])
+                + (
+                    east[z] * source[base + z, row + 2 : row + 10, :]
+                    + west[z] * source[base + z, row - 2 : row + 6, :]
+                )
+                + force[base + z]
+            )
+        energy, moisture = stepped
+        excess = jnp.maximum(moisture - jnp.exp2(energy), 0.0)
+        results.append((energy + rates[0] * excess, moisture - rates[1] * excess))
+    return results
+
+
+def sweep(levels, many, work, keep):
+    def body(i, carry):
+        zs = [i * many + k for k in range(many)]
+        found = [work(z, jnp.maximum(z - 1, 0), jnp.minimum(z + 1, levels - 1)) for z in zs]
+        for z, results in zip(zs, found):
+            keep(z, results)
+        return carry
+
+    lax.fori_loop(0, levels // many, body, 0)
+    for z in range(levels // many * many, levels):
+        keep(z, work(z, max(z - 1, 0), min(z + 1, levels - 1)))
+
+
+NARROW = ((10, 18, 22), (12, 20), (14, 18), (16,))
+MANY = (9, 29, 29, 29)
+
+
+def inner_kernel(parity, force, east, west, rate, own, near0, near1, edges, even, odd):
+    levels = east.shape[0]
+    rates = (rate[0], rate[1])
+
+    def fill(left, right):
+        def body(z, carry):
+            for slab, first in ((left, 4), (own, 8), (right, 12)):
+                place(slab, first, even, z)
+            return carry
+
+        lax.fori_loop(0, levels, body, 0, unroll=2)
+
+    @pl.when(parity[0] == 0)
+    def _():
+        fill(near1, near0)
+
+    @pl.when(parity[0] == 1)
+    def _():
+        fill(near0, near1)
+
+    def copy_edges(t, source):
+        def body(i, carry):
+            edges[t, i, 0:4, :] = source[i, 8 + 2 * t : 12 + 2 * t, :]
+            edges[t, i, 4:8, :] = source[i, 28 - 2 * t : 32 - 2 * t, :]
+            if t == 0:
+                edges[5, i] = source[i, 16:24, :]
+            return carry
+
+        lax.fori_loop(0, 2 * levels, body, 0, unroll=4)
+
+    copy_edges(0, even)
+    for t, starts in enumerate(NARROW):
+        source, target = (even, odd) if t % 2 == 0 else (odd, even)
+
+        def keep(z, results, target=target, starts=starts):
+            for row, pair in zip(starts, results):
+                for f, value in enumerate(pair):
+                    target[f * levels + z, row : row + 8, :] = value
+
+        def work(z, below, above, source=source, starts=starts):
+            return march(force, east, west, rates, source, z, below, above, starts)
+
+        sweep(levels, MANY[t], work, keep)
+        copy_edges(t + 1, target)
+
+
+def outer_kernel(parity, force, east, west, rate, far0, far1, edges, ended, change, even, odd, sums):
+    levels = east.shape[0]
+    rates = (rate[0], rate[1])
+    share = change.shape[1] // 2
     sums[...] = jnp.zeros_like(sums)
 
-    def place(z, carry):
-        for f in range(fields):
-            for c in range(lane_tiles):
-                for s, slab in enumerate(slabs):
-                    value = slab[f * levels + z, c * cells : (c + 1) * cells, :]
-                    value = GROWTH * value - 1.0 if f == 0 else value + sat_scale
-                    even[f, z, c, s * cells : (s + 1) * cells, :] = value
+    def fill(left, right):
+        def body(z, carry):
+            place(left, 0, even, z)
+            place(right, 16, even, z)
+            for f in range(2):
+                i = f * levels + z
+                even[i, 8:12, :] = edges[0, i, 0:4, :]
+                even[i, 28:32, :] = edges[0, i, 4:8, :]
+            return carry
+
+        lax.fori_loop(0, levels, body, 0, unroll=2)
+
+    @pl.when(parity[0] == 0)
+    def _():
+        fill(far1, far0)
+
+    @pl.when(parity[0] == 1)
+    def _():
+        fill(far0, far1)
+
+    for t in range(4):
+        source, target = (even, odd) if t % 2 == 0 else (odd, even)
+        starts = (2 * t + 2, 30 - 2 * t)
+
+        def keep(z, results, t=t, target=target, starts=starts):
+            for f in range(2):
+                i = f * levels + z
+                for row, pair in zip(starts, results):
+                    target[i, row : row + 8, :] = pair[f]
+                target[i, 10 + 2 * t : 14 + 2 * t, :] = edges[t + 1, i, 0:4, :]
+                target[i, 26 - 2 * t : 30 - 2 * t, :] = edges[t + 1, i, 4:8, :]
+
+        def work(z, below, above, source=source, starts=starts):
+            return march(force, east, west, rates, source, z, below, above, starts)
+
+        sweep(levels, 29, work, keep)
+    for t, starts in enumerate(NARROW):
+        source, target = (even, odd) if t % 2 == 0 else (odd, even)
+
+        def keep(z, results, t=t, target=target, starts=starts):
+            for row, pair in zip(starts, results):
+                for f, value in enumerate(pair):
+                    i = f * levels + z
+                    if t < len(NARROW) - 1:
+                        target[i, row : row + 8, :] = value
+                        continue
+                    grown = value - edges[5, i]
+                    ended[i] = (value + 1.0) * (1.0 / GROWTH) if f == 0 else value - sat_scale
+                    grown = grown + pltpu.roll(grown, 2, 0)
+                    grown = grown + pltpu.roll(grown, 4, 0)
+                    for c in range(2):
+                        sums[f, c, pl.ds(z, 1), :] = grown[c : c + 1, :]
+
+        def work(z, below, above, source=source, starts=starts):
+            return march(force, east, west, rates, source, z, below, above, starts)
+
+        sweep(levels, MANY[t], work, keep)
+
+    for f in range(2):
+        scale = 1.0 / GROWTH if f == 0 else 1.0
+        for c in range(2):
+            for g in range(change.shape[0]):
+                change[g, f * share : (f + 1) * share, c * LANES : (c + 1) * LANES] = (
+                    scale * sums[f, c, g * share : (g + 1) * share, :]
+                )
+
+
+def finish_kernel(ended, final):
+    def body(i, carry):
+        for c in range(2):
+            final[i, 4 * c : 4 * c + 4, :] = ended[i, pl.ds(c, 4, stride=2), :]
         return carry
 
-    lax.fori_loop(0, levels, place, 0)
-    rates = [[jnp.broadcast_to(rate[f, c, :1, :], (8, LANES)) for c in range(lane_tiles)] for f in range(2)]
-
-    def at_level(step, source, z, below, above):
-        results = []
-        for c in range(lane_tiles):
-            wide = [jnp.broadcast_to(w[c, pl.ds(z, 1), :], (8, LANES)) for w in (east, west)]
-            push = [jnp.broadcast_to(force[f, c, pl.ds(z, 1), :], (8, LANES)) for f in range(fields)]
-            for row in BLOCKS[step]:
-                rows = slice(row, row + 8)
-                stepped = []
-                for f in range(fields):
-                    stepped.append(
-                        (1.0 - 2.0 * diffuse_x - 2.0 * diffuse_z) * source[f, z, c, rows, :]
-                        + diffuse_z * (source[f, below, c, rows, :] + source[f, above, c, rows, :])
-                        + (
-                            wide[0] * source[f, z, c, row + 1 : row + 9, :]
-                            + wide[1] * source[f, z, c, row - 1 : row + 7, :]
-                        )
-                        + push[f]
-                    )
-                energy, moisture = stepped
-                excess = jnp.maximum(moisture - jnp.exp2(energy), 0.0)
-                results.append((c, row, energy + rates[1][c] * excess, moisture - rates[0][c] * excess))
-        return results
-
-    def store(step, target, z, results):
-        for c, row, energy, moisture in results:
-            if step < STEPS - 1:
-                target[0, z, c, row : row + 8, :] = energy
-                target[1, z, c, row : row + 8, :] = moisture
-                continue
-            energy = (energy + 1.0) * (1.0 / GROWTH)
-            moisture = moisture - sat_scale
-            for f, now in enumerate((energy, moisture)):
-                now = now[:cells]
-                start = own[f * levels + z, c * cells : (c + 1) * cells, :]
-                final[f * levels + z, c * cells : (c + 1) * cells, :] = now
-                sums[f, c, pl.ds(z, 1), :] = jnp.sum(now - start, axis=0, keepdims=True)
-
-    for step in range(STEPS):
-        source, target = (even, odd) if step % 2 == 0 else (odd, even)
-        many = GROUPS[step]
-
-        def body(i, carry, step=step, source=source, target=target, many=many):
-            zs = [i * many + k for k in range(many)]
-            found = [
-                at_level(step, source, z, jnp.maximum(z - 1, 0), jnp.minimum(z + 1, levels - 1))
-                for z in zs
-            ]
-            for z, results in zip(zs, found):
-                store(step, target, z, results)
-            return carry
-
-        lax.fori_loop(0, levels // many, body, 0)
-        for z in range(levels // many * many, levels):
-            store(step, target, z, at_level(step, source, z, max(z - 1, 0), min(z + 1, levels - 1)))
-    for f in range(fields):
-        for c in range(lane_tiles):
-            for g in range(change.shape[0]):
-                change[g, f * share : (f + 1) * share, c * LANES : (c + 1) * LANES] = sums[
-                    f, c, g * share : (g + 1) * share, :
-                ]
+    lax.fori_loop(0, final.shape[0], body, 0, unroll=4)
 
 
 def return_kernel(inverse, parts, lands, sent):
@@ -255,20 +362,22 @@
                 tendency[start : start + here, :] = every[g, f * share : f * share + here, :]
 
 
-def call(kernel, outs, scratch=(), scalars=0, inputs=0):
+def call(kernel, outs, scratch=(), scalars=0, inputs=0, limit=16):
     return pl.pallas_call(
         kernel,
         out_shape=outs,
         in_specs=[SMEM] * scalars + [VMEM] * inputs,
         out_specs=jax.tree.map(lambda _: VMEM, outs),
         scratch_shapes=list(scratch),
-        compiler_params=pltpu.CompilerParams(vmem_limit_bytes=16 * 1024 * 1024),
-    )
-
-
-def shifted(x, by):
+        compiler_params=pltpu.CompilerParams(vmem_limit_bytes=limit * 1024 * 1024),
+    )
+
+
+def swapped(x, odd):
     peers = lax.axis_size("grp")
-    return lax.ppermute(x, "grp", [(i, (i + by) % peers) for i in range(peers)])
+    return lax.ppermute(
+        x, "grp", [(i, (i + 1 if i % 2 == odd else i - 1) % peers) for i in range(peers)]
+    )
 
 
 def traded(x, axis):
@@ -296,7 +405,7 @@
     S = jax.ShapeDtypeStruct
     me = lax.axis_index("col").reshape(1)
     owners = owner_map.reshape(-1, LANES)
-    left1, right1 = shifted(crm_state, 1), shifted(crm_state, -1)
+    near0, near1 = swapped(crm_state, 0), swapped(crm_state, 1)
     tiles = capacity + capacity // 2
     packed, picks = call(
         pack_kernel,
@@ -304,31 +413,38 @@
         (),
         1,
         3,
+        60,
     )(me, owners, profiles.T, courant.T)
     got = traded(packed.reshape(col_count, 1, tiles * LANES), "col").reshape(packed.shape)
     lands = call(landing_kernel, S((capacity * col_count, columns), bf16), (), 1, 1)(me, owners)
-    left2, right2 = shifted(left1, 1), shifted(right1, -1)
+    far0, far1 = swapped(near1, 0), swapped(near0, 1)
+    lines = fields * levels
     forces = call(
         forcing_kernel,
         (
-            S((fields, lane_tiles, tall, LANES), f32),
-            S((lane_tiles, tall, LANES), f32),
-            S((lane_tiles, tall, LANES), f32),
-            S((2, lane_tiles, 8, LANES), f32),
+            S((lines, 8, LANES), f32),
+            S((levels, 8, LANES), f32),
+            S((levels, 8, LANES), f32),
+            S((2, 8, LANES), f32),
         ),
-        (),
+        [pltpu.VMEM((lane_tiles, 3 * LANES // 2, LANES), f32)],
         0,
         3,
     )(got, lands, cloud_flags.reshape(1, columns))
-    slabs = [flat(x) for x in (crm_state, left1, right1, left2, right2)]
-    rows, change = call(
-        steps_kernel,
-        (S(slabs[0].shape, f32), S((pieces, 2 * share, columns), f32)),
-        [pltpu.VMEM((fields, levels, lane_tiles, 24, LANES), f32)] * 2
-        + [pltpu.VMEM((fields, lane_tiles, tall, LANES), f32)],
-        0,
-        9,
-    )(*forces, *slabs)
+    parity = (lax.axis_index("grp") % 2).reshape(1)
+    own = flat(crm_state)
+    state = pltpu.VMEM((lines, 40, LANES), f32)
+    edges = call(inner_kernel, S((6, lines, 8, LANES), f32), [state, state], 1, 7)(
+        parity, *forces, own, flat(near0), flat(near1)
+    )
+    ended, change = call(
+        outer_kernel,
+        (S(own.shape, f32), S((pieces, 2 * share, columns), f32)),
+        [state, state, pltpu.VMEM((fields, lane_tiles, tall, LANES), f32)],
+        1,
+        7,
+    )(parity, *forces, flat(far0), flat(far1), edges)
+    rows = call(finish_kernel, S(own.shape, f32), (), 0, 1)(ended)
     rows = rows.reshape(fields, levels, lane_tiles, cells, LANES).transpose(0, 1, 3, 2, 4)
     crm_final = rows.reshape(crm_state.shape)
     parts = traded(change, "grp")

time: 123 us -> 116 us (0.943)
  blocking collectives: 52.8 us -> 37.4 us
  waiting for transfers between devices: 12.1 us -> 17.9 us
  starting transfers between devices: 38.8 us -> 40.8 us
    all_to_all x3 -> x2, blocking collectives: 52.8 us -> 37.4 us  [traded(): return lax.all_to_all(x, axis, split_axis=0, concat_axis=0, tiled=True)]
    all_to_all x1 -> x2, waiting for transfers between devices: 6.42 us -> 17.9 us  [traded(): return lax.all_to_all(x, axis, split_axis=0, concat_axis=0, tiled=True)]
    ppermute x4, waiting for transfers between devices: 5.66 us -> 0.01 us  [swapped(): lax.ppermute(x, 'grp', [(i, (i + 1 if i % 2 == odd else i - 1) % peers) f...]
    all_to_all x1 -> x2, starting transfers between devices: 11.2 us -> 14.6 us  [traded(): return lax.all_to_all(x, axis, split_axis=0, concat_axis=0, tiled=True)]
    ppermute x4, starting transfers between devices: 27.6 us -> 26.2 us  [swapped(): lax.ppermute(x, 'grp', [(i, (i + 1 if i % 2 == odd else i - 1) % peers) f...]
    pallas_call x2 -> x4, Pallas kernels: 11.4 us -> 10.1 us  [the longest x1 4.9 us: on_device(): call(outer_kernel, (S(own.shape, f32), S((pieces, 2 * share, columns), f3...]
    unnamed x12 -> x8, local copies, waits for them, and re-layouts: 2.59 us -> 2.54 us
  transfers between devices with their start and end apart: 5 -> 6, of which waited for: 3 -> 2; matrix products, arithmetic and copies ran while one was open for 0% -> 0% of each run, Pallas kernels for 2% -> 7%
where the time goes in v3:
time: 116 us; the launch traced here: 114 us
  starting transfers between devices  40.8 us (35%)
  blocking collectives  37.4 us (32%)
  waiting for transfers between devices  17.9 us (15%)
  Pallas kernels  14.8 us (13%)
  local copies, waits for them, and re-layouts  2.54 us (2%)
    all_to_all x2, blocking collectives, traded(): return lax.all_to_all(x, axis, split_axis=0, concat_axis=0, tiled=True)  37.4 us
    ppermute x4, starting transfers between devices, swapped(): lax.ppermute(x, 'grp', [(i, (i + 1 if i % 2 == odd else i - 1) % peers) f...  26.2 us
    all_to_all x2, waiting for transfers between devices, traded(): return lax.all_to_all(x, axis, split_axis=0, concat_axis=0, tiled=True)  17.9 us
    all_to_all x2, starting transfers between devices, traded(): return lax.all_to_all(x, axis, split_axis=0, concat_axis=0, tiled=True)  14.6 us
    pallas_call x1, Pallas kernels, on_device(): call(outer_kernel, (S(own.shape, f32), S((pieces, 2 * share, columns), f3...  4.9 us
    pallas_call x1, Pallas kernels, on_device(): call(inner_kernel, S((6, lines, 8, LANES), f32), [state, state], 1, 7)  3.48 us
    unnamed x8, local copies, waits for them, and re-layouts  2.54 us
  transfers between devices with their start and end apart: 6, of which 2 were waited for; matrix products, arithmetic and copies ran while one was open for 0% of the time, Pallas kernels for 7%

profile of v3, /device:TPU:1, one launch (start us, length us, event | category | flops | bytes accessed | tf_op | source)
XLA Modules:
  0.0 114.3 jit_solution(1408984573122936018)
XLA Ops:
  0.6 18.8 %collective-permute-start = (f32[2,58,4,256]{3,2,1,0:T(4,128)}, f32[2,58,4,256]{3,2,1,0:T(4,128)S(1)}, u32[]{:S(2)}, u32[]{:S(2)}) collective-permute-start(f32[2,58,4,256]{3,2,1,0:T(4,128)} %param.9), channel_id=1, source_target_pairs={{0,15},{1,2},{2,1},{3,4},{4,3},{5,6},{6,5},{7,8},{8,7},{9,10},{10,... | collective-permute-start | bytes 1425416 | tf_op jit(solution)/shard_map/ppermute | solution.py:378
  19.4 1.9 %collective-permute-start.2 = (f32[2,58,4,256]{3,2,1,0:T(4,128)}, f32[2,58,4,256]{3,2,1,0:T(4,128)S(1)}, u32[]{:S(2)}, u32[]{:S(2)}) collective-permute-start(f32[2,58,4,256]{3,2,1,0:T(4,128)} %param.9), channel_id=1, source_target_pairs={{0,1},{1,0},{2,3},{3,2},{4,5},{5,4},{6,7},{7,6},{8,9},{9,8},{10,11... | collective-permute-start | bytes 1425416 | tf_op jit(solution)/shard_map/ppermute | solution.py:378
  21.3 2.3 %shard_map.68 = (f32[576,128]{1,0:T(8,128)}, bf16[384,256]{1,0:T(8,128)(2,1)}) custom-call(s32[1]{0:T(128)} %bitcast.1.me, s32[128,128]{1,0:T(8,128)} %bitcast.49, f32[116,256]{1,0:T(8,128)} %bitcast.56, f32[58,256]{1,0:T(8,128)} %bitcast.58), custom_call_target="tpu_custom_call" | custom-call | tf_op jit(solution)/shard_map/pallas_call | solution.py:410
  23.6 11.1 %all-to-all-start = ((f32[64,1,1152]{2,1,0:T(1,128)}), f32[64,1,1152]{2,1,0:T(1,128)S(1)}, u32[]{:S(2)}, u32[]{:S(2)}) async-start(f32[64,1,1152]{2,1,0:T(1,128)} %bitcast.55), calls=%async_computation | async-start | bytes 589824 | tf_op jit(solution)/shard_map/all_to_all | solution.py:384
  34.7 0.0 collective-permute-done
  34.7 3.6 %collective-permute-start.1 = (f32[2,58,4,256]{3,2,1,0:T(4,128)S(1)}, f32[2,58,4,256]{3,2,1,0:T(4,128)S(1)}, u32[]{:S(2)}, u32[]{:S(2)}) collective-permute-start(f32[2,58,4,256]{3,2,1,0:T(4,128)S(1)} %collective-permute-done), channel_id=1, source_target_pairs={{0,1},{1,0},{2,3},{3,2},{4,5},{5,4},{6,7},{7,6},{8,9},{9,8},{10,11... | collective-permute-start | bytes 1425416 | tf_op jit(solution)/shard_map/ppermute | solution.py:378
  38.3 0.0 collective-permute-done.2
  38.4 1.9 %collective-permute-start.3 = (f32[2,58,4,256]{3,2,1,0:T(4,128)S(1)}, f32[2,58,4,256]{3,2,1,0:T(4,128)S(1)}, u32[]{:S(2)}, u32[]{:S(2)}) collective-permute-start(f32[2,58,4,256]{3,2,1,0:T(4,128)S(1)} %collective-permute-done.2), channel_id=1, source_target_pairs={{0,15},{1,2},{2,1},{3,4},{4,3},{5,6},{6,5},{7,8},{8,7},{9,10},{10,... | collective-permute-start | bytes 1425416 | tf_op jit(solution)/shard_map/ppermute | solution.py:378
  40.3 0.0 copy-start.1
  40.3 0.8 copy-done.1
  41.1 0.3 shard_map.69.lands
  41.4 6.9 %all-to-all-done = f32[64,1,1152]{2,1,0:T(1,128)S(1)} async-done(((f32[64,1,1152]{2,1,0:T(1,128)}), f32[64,1,1152]{2,1,0:T(1,128)S(1)}, u32[]{:S(2)}, u32[]{:S(2)}) %all-to-all-start) | async-done | bytes 294944 | tf_op jit(solution)/shard_map/all_to_all | solution.py:384
  48.4 0.0 copy-start.3
  48.4 0.7 copy-done.3
  49.0 0.7 shard_map.70
  49.8 0.0 copy-start
  49.8 1.0 copy-done
  50.8 3.5 %shard_map.71.edges = f32[6,116,8,128]{3,2,1,0:T(8,128)S(1)} custom-call(s32[1]{0:T(128)} %bitcast.parity, f32[116,8,128]{2,1,0:T(8,128)S(1)} %get-tuple-element.11.force, f32[58,8,128]{2,1,0:T(8,128)S(1)} %get-tuple-element.12.east, f32[58,8,128]{2,1,0:T(8,128)S(1)} %get-tuple-element.13.west, f32[2,8,128]{2,1,0:T(8,128)S(1)} %get-tuple-element.14.rate, ...), custom_call_target="tpu_custom_call" | custom-call | tf_op jit(solution)/shard_map/pallas_call | solution.py:437
  54.3 0.0 copy-start.2
  54.3 0.0 collective-permute-done.1
  54.3 0.0 collective-permute-done.3
  54.3 4.9 %shard_map.72 = (f32[116,8,128]{2,1,0:T(8,128)S(1)}, f32[16,8,256]{2,1,0:T(8,128)S(1)}) custom-call(s32[1]{0:T(128)} %bitcast.parity, f32[116,8,128]{2,1,0:T(8,128)S(1)} %get-tuple-element.11.force, f32[58,8,128]{2,1,0:T(8,128)S(1)} %get-tuple-element.12.east, f32[58,8,128]{2,1,0:T(8,128)S(1)} %get-tuple-element.13.west, ...), custom_call_target="tpu_custom_call" | custom-call | tf_op jit(solution)/shard_map/pallas_call | solution.py:440
  59.2 17.1 %all_to_all.20.parts = f32[16,8,256]{2,1,0:T(8,128)S(1)} all-to-all(f32[16,8,256]{2,1,0:T(8,128)S(1)} %get-tuple-element.15), channel_id=1, replica_groups=mesh['col'=64,'grp'=16] {'grp'}, dimensions={0} | all-to-all | bytes 262144 | tf_op jit(solution)/shard_map/all_to_all | solution.py:384
  76.3 0.3 shard_map.73
  76.7 20.3 %all_to_all.21 = f32[64,1,128]{2,1,0:T(1,128)S(1)} all-to-all(f32[64,1,128]{2,1,0:T(1,128)S(1)} %bitcast.51), channel_id=1, replica_groups=mesh['col'=64,'grp'=16] {'col'}, dimensions={0} | all-to-all | bytes 65536 | tf_op jit(solution)/shard_map/all_to_all | solution.py:384
  97.0 0.0 copy-done.2
  97.0 1.2 %shard_map.74 = f32[16,8,256]{2,1,0:T(8,128)} custom-call(f32[64,128]{1,0:T(8,128)S(1)} %bitcast.52, bf16[384,256]{1,0:T(8,128)(2,1)S(1)} %copy-done.2), custom_call_target="tpu_custom_call" | custom-call | tf_op jit(solution)/shard_map/pallas_call | solution.py:454
  98.2 3.5 %all-to-all-start.3 = ((f32[16,8,256]{2,1,0:T(8,128)}), f32[16,8,256]{2,1,0:T(8,128)S(1)}, u32[]{:S(2)}, u32[]{:S(2)}) async-start(f32[16,8,256]{2,1,0:T(8,128)} %shard_map.74), calls=%async_computation.3 | async-start | bytes 262144 | tf_op jit(solution)/shard_map/all_to_all | solution.py:384
  101.7 1.0 shard_map.76
  102.7 10.9 %all-to-all-done.3.every = f32[16,8,256]{2,1,0:T(8,128)S(1)} async-done(((f32[16,8,256]{2,1,0:T(8,128)}), f32[16,8,256]{2,1,0:T(8,128)S(1)}, u32[]{:S(2)}, u32[]{:S(2)}) %all-to-all-start.3) | async-done | bytes 131104 | tf_op jit(solution)/shard_map/all_to_all | solution.py:384
  113.6 0.7 shard_map.75
Async XLA Ops:
  0.6 34.1 %collective-permute-start = (f32[2,58,4,256]{3,2,1,0:T(4,128)}, f32[2,58,4,256]{3,2,1,0:T(4,128)S(1)}, u32[]{:S(2)}, u32[]{:S(2)}) collective-permute-start(f32[2,58,4,256]{3,2,1,0:T(4,128)} %param.9), channel_id=1, source_target_pairs={{0,15},{1,2},{2,1},{3,4},{4,3},{5,6},{6,5},{7,8},{8,7},{9,10},{10,... | collective-permute-start | bytes 1425416 | tf_op jit(solution)/shard_map/ppermute | solution.py:378
  19.4 18.9 %collective-permute-start.2 = (f32[2,58,4,256]{3,2,1,0:T(4,128)}, f32[2,58,4,256]{3,2,1,0:T(4,128)S(1)}, u32[]{:S(2)}, u32[]{:S(2)}) collective-permute-start(f32[2,58,4,256]{3,2,1,0:T(4,128)} %param.9), channel_id=1, source_target_pairs={{0,1},{1,0},{2,3},{3,2},{4,5},{5,4},{6,7},{7,6},{8,9},{9,8},{10,11... | collective-permute-start | bytes 1425416 | tf_op jit(solution)/shard_map/ppermute | solution.py:378
  23.6 24.8 %all-to-all-start = ((f32[64,1,1152]{2,1,0:T(1,128)}), f32[64,1,1152]{2,1,0:T(1,128)S(1)}, u32[]{:S(2)}, u32[]{:S(2)}) async-start(f32[64,1,1152]{2,1,0:T(1,128)} %bitcast.55), calls=%async_computation | async-start | bytes 589824 | tf_op jit(solution)/shard_map/all_to_all | solution.py:384
  34.7 19.6 %collective-permute-start.1 = (f32[2,58,4,256]{3,2,1,0:T(4,128)S(1)}, f32[2,58,4,256]{3,2,1,0:T(4,128)S(1)}, u32[]{:S(2)}, u32[]{:S(2)}) collective-permute-start(f32[2,58,4,256]{3,2,1,0:T(4,128)S(1)} %collective-permute-done), channel_id=1, source_target_pairs={{0,1},{1,0},{2,3},{3,2},{4,5},{5,4},{6,7},{7,6},{8,9},{9,8},{10,11... | collective-permute-start | bytes 1425416 | tf_op jit(solution)/shard_map/ppermute | solution.py:378
  38.4 16.0 %collective-permute-start.3 = (f32[2,58,4,256]{3,2,1,0:T(4,128)S(1)}, f32[2,58,4,256]{3,2,1,0:T(4,128)S(1)}, u32[]{:S(2)}, u32[]{:S(2)}) collective-permute-start(f32[2,58,4,256]{3,2,1,0:T(4,128)S(1)} %collective-permute-done.2), channel_id=1, source_target_pairs={{0,15},{1,2},{2,1},{3,4},{4,3},{5,6},{6,5},{7,8},{8,7},{9,10},{10,... | collective-permute-start | bytes 1425416 | tf_op jit(solution)/shard_map/ppermute | solution.py:378
  40.3 0.8 copy-start.1
  48.4 0.7 copy-start.3
  49.8 1.0 copy-start
  54.3 42.7 %copy-start.2 = (bf16[384,256]{1,0:T(8,128)(2,1)S(1)}, bf16[384,256]{1,0:T(8,128)(2,1)}, u32[]{:S(2)}) copy-start(bf16[384,256]{1,0:T(8,128)(2,1)} %get-tuple-element.16.picks) | copy-start | bytes 589828
  98.2 15.4 %all-to-all-start.3 = ((f32[16,8,256]{2,1,0:T(8,128)}), f32[16,8,256]{2,1,0:T(8,128)S(1)}, u32[]{:S(2)}, u32[]{:S(2)}) async-start(f32[16,8,256]{2,1,0:T(8,128)} %shard_map.74), calls=%async_computation.3 | async-start | bytes 262144 | tf_op jit(solution)/shard_map/all_to_all | solution.py:384

commit v4 on v3

--- a/solution.py
+++ b/solution.py
@@ -47,21 +47,25 @@
     return jnp.concatenate([left, right], axis=1)
 
 
-def pack_kernel(me, owners, prof, cour, packed, picks):
+def chosen_slots(me, owners, peers, slots):
+    mine = [owners[pl.ds(2 * me[0] + i, 1), :] for i in range(2)]
+    mine = jnp.concatenate(mine, axis=1)
+    columns = mine.shape[1]
+    hits = lax.broadcasted_iota(jnp.int32, (peers, columns), 0) == mine // columns
+    order = earlier(hits, columns)
+    return jnp.concatenate(
+        [jnp.where(hits & (order == k), 1.0, 0.0) for k in range(slots)], axis=0
+    ).astype(jnp.bfloat16)
+
+
+def pack_kernel(me, owners, prof, cour, packed):
     feats, columns = prof.shape
     levels = cour.shape[0]
     peers = owners.shape[0] * LANES // columns
-    slots = picks.shape[0] // peers
     tiles = packed.shape[0] // peers
+    slots = tiles * 2 // 3
     half = LANES // 2
-    mine = [owners[pl.ds(2 * me[0] + i, 1), :] for i in range(2)]
-    target = jnp.concatenate(mine, axis=1) // columns
-    hits = lax.broadcasted_iota(jnp.int32, (peers, columns), 0) == target
-    order = earlier(hits, columns)
-    chosen = jnp.concatenate(
-        [jnp.where(hits & (order == k), 1.0, 0.0) for k in range(slots)], axis=0
-    ).astype(jnp.bfloat16)
-    picks[...] = chosen
+    chosen = chosen_slots(me, owners, peers, slots)
     gap = jnp.zeros((half - levels, columns), jnp.float32)
     wind = jnp.concatenate([cour[...], gap], axis=0)
     blank = jnp.zeros_like(wind)
@@ -78,23 +82,38 @@
         packed[pl.ds(slots + j, peers, stride=tiles), :] = low + high
 
 
-def landing_kernel(me, owners, lands):
+def landing_kernel(me, owners, flags, own, lands, picks, rate, start):
     columns = lands.shape[1]
     peers = owners.shape[0] * LANES // columns
     slots = lands.shape[0] // peers
-    own = rows_of(owners, peers)
-    hits = own // columns == me[0]
+    picks[...] = chosen_slots(me, owners, peers, slots)
+    spans = rows_of(owners, peers)
+    hits = spans // columns == me[0]
     order = earlier(hits, columns)
-    local = (own % columns + 1).astype(jnp.float32)
-    place = lax.broadcasted_iota(jnp.int32, (peers, columns), 1).astype(jnp.float32)
+    local = (spans % columns + 1).astype(jnp.float32)
+    spot_of = lax.broadcasted_iota(jnp.int32, (peers, columns), 1).astype(jnp.float32)
     for k in range(slots):
         spot = jnp.sum(jnp.where(hits & (order == k), local, 0.0), axis=1, keepdims=True)
-        lands[k * peers : (k + 1) * peers, :] = jnp.where(spot - 1.0 == place, 1.0, 0.0).astype(
+        lands[k * peers : (k + 1) * peers, :] = jnp.where(spot - 1.0 == spot_of, 1.0, 0.0).astype(
             jnp.bfloat16
         )
-
-
-def forcing_kernel(got, lands, flags, force, east, west, rate, rows):
+    even = lax.broadcasted_iota(jnp.int32, (8, LANES), 0) % 2 == 0
+    fraction = cond_rate * flags[...].astype(jnp.float32)
+    first, second = (
+        jnp.broadcast_to(fraction[:, c * LANES : (c + 1) * LANES], (8, LANES)) for c in (0, 1)
+    )
+    fraction = jnp.where(even, first, second)
+    rate[0] = (latent_gain * GROWTH) * fraction
+    rate[1] = fraction
+
+    def body(z, carry):
+        place(own, 0, start, z)
+        return carry
+
+    lax.fori_loop(0, own.shape[0] // 2, body, 0, unroll=2)
+
+
+def forcing_kernel(got, lands, force, east, west, rows):
     columns = lands.shape[1]
     tiles = 9
     peers = got.shape[0] // tiles
@@ -133,13 +152,6 @@
         return carry
 
     lax.fori_loop(0, levels, weave, 0, unroll=2)
-    fraction = cond_rate * flags[...].astype(jnp.float32)
-    first, second = (
-        jnp.broadcast_to(fraction[:, c * LANES : (c + 1) * LANES], (8, LANES)) for c in (0, 1)
-    )
-    fraction = jnp.where(even, first, second)
-    rate[0] = (latent_gain * GROWTH) * fraction
-    rate[1] = fraction
 
 
 def place(slab, first, target, z):
@@ -191,14 +203,16 @@
 MANY = (9, 29, 29, 29)
 
 
-def inner_kernel(parity, force, east, west, rate, own, near0, near1, edges, even, odd):
+def inner_kernel(parity, force, east, west, rate, start, near0, near1, edges, even, odd):
     levels = east.shape[0]
     rates = (rate[0], rate[1])
 
     def fill(left, right):
         def body(z, carry):
-            for slab, first in ((left, 4), (own, 8), (right, 12)):
-                place(slab, first, even, z)
+            place(left, 4, even, z)
+            place(right, 12, even, z)
+            for i in (z, levels + z):
+                even[i, 16:24, :] = start[i]
             return carry
 
         lax.fori_loop(0, levels, body, 0, unroll=2)
@@ -215,8 +229,6 @@
         def body(i, carry):
             edges[t, i, 0:4, :] = source[i, 8 + 2 * t : 12 + 2 * t, :]
             edges[t, i, 4:8, :] = source[i, 28 - 2 * t : 32 - 2 * t, :]
-            if t == 0:
-                edges[5, i] = source[i, 16:24, :]
             return carry
 
         lax.fori_loop(0, 2 * levels, body, 0, unroll=4)
@@ -237,48 +249,75 @@
         copy_edges(t + 1, target)
 
 
-def outer_kernel(parity, force, east, west, rate, far0, far1, edges, ended, change, even, odd, sums):
+def outer_side(left, far, force, east, west, rates, edges, even, odd):
+    levels = east.shape[0]
+    part = slice(0, 4) if left else slice(4, 8)
+
+    def body(z, carry):
+        place(far, 0 if left else 16, even, z)
+        row = 8 if left else 28
+        for i in (z, levels + z):
+            even[i, row : row + 4, :] = edges[0, i, part, :]
+        return carry
+
+    lax.fori_loop(0, levels, body, 0, unroll=2)
+    for t in range(4):
+        source, target = (even, odd) if t % 2 == 0 else (odd, even)
+        start = 2 * t + 2 if left else 30 - 2 * t
+        row = 10 + 2 * t if left else 26 - 2 * t
+
+        def keep(z, results, t=t, target=target, start=start, row=row):
+            for f in range(2):
+                i = f * levels + z
+                target[i, start : start + 8, :] = results[0][f]
+                target[i, row : row + 4, :] = edges[t + 1, i, part, :]
+
+        def work(z, below, above, source=source, start=start):
+            return march(force, east, west, rates, source, z, below, above, (start,))
+
+        sweep(levels, 29, work, keep)
+
+
+def side_kernel(parity, force, east, west, rate, far, edges, strip, even, odd):
+    rates = (rate[0], rate[1])
+
+    def run(left):
+        outer_side(left, far, force, east, west, rates, edges, even, odd)
+        row = 8 if left else 24
+
+        def body(i, carry):
+            strip[i] = even[i, row : row + 8, :]
+            return carry
+
+        lax.fori_loop(0, strip.shape[0], body, 0, unroll=4)
+
+    pl.when(parity[0] == 0)(lambda: run(False))
+    pl.when(parity[0] == 1)(lambda: run(True))
+
+
+def outer_kernel(
+    parity, force, east, west, rate, far, edges, strip, first, ended, change, even, odd, sums
+):
     levels = east.shape[0]
     rates = (rate[0], rate[1])
     share = change.shape[1] // 2
     sums[...] = jnp.zeros_like(sums)
 
-    def fill(left, right):
-        def body(z, carry):
-            place(left, 0, even, z)
-            place(right, 16, even, z)
-            for f in range(2):
-                i = f * levels + z
-                even[i, 8:12, :] = edges[0, i, 0:4, :]
-                even[i, 28:32, :] = edges[0, i, 4:8, :]
+    def run(left):
+        outer_side(left, far, force, east, west, rates, edges, even, odd)
+        row = 24 if left else 8
+        inward = 20 if left else 16
+        part = slice(4, 8) if left else slice(0, 4)
+
+        def body(i, carry):
+            even[i, row : row + 8, :] = strip[i]
+            even[i, inward : inward + 4, :] = edges[4, i, part, :]
             return carry
 
-        lax.fori_loop(0, levels, body, 0, unroll=2)
-
-    @pl.when(parity[0] == 0)
-    def _():
-        fill(far1, far0)
-
-    @pl.when(parity[0] == 1)
-    def _():
-        fill(far0, far1)
-
-    for t in range(4):
-        source, target = (even, odd) if t % 2 == 0 else (odd, even)
-        starts = (2 * t + 2, 30 - 2 * t)
-
-        def keep(z, results, t=t, target=target, starts=starts):
-            for f in range(2):
-                i = f * levels + z
-                for row, pair in zip(starts, results):
-                    target[i, row : row + 8, :] = pair[f]
-                target[i, 10 + 2 * t : 14 + 2 * t, :] = edges[t + 1, i, 0:4, :]
-                target[i, 26 - 2 * t : 30 - 2 * t, :] = edges[t + 1, i, 4:8, :]
-
-        def work(z, below, above, source=source, starts=starts):
-            return march(force, east, west, rates, source, z, below, above, starts)
-
-        sweep(levels, 29, work, keep)
+        lax.fori_loop(0, 2 * levels, body, 0, unroll=4)
+
+    pl.when(parity[0] == 0)(lambda: run(True))
+    pl.when(parity[0] == 1)(lambda: run(False))
     for t, starts in enumerate(NARROW):
         source, target = (even, odd) if t % 2 == 0 else (odd, even)
 
@@ -289,7 +328,7 @@
                     if t < len(NARROW) - 1:
                         target[i, row : row + 8, :] = value
                         continue
-                    grown = value - edges[5, i]
+                    grown = value - first[i]
                     ended[i] = (value + 1.0) * (1.0 / GROWTH) if f == 0 else value - sat_scale
                     grown = grown + pltpu.roll(grown, 2, 0)
                     grown = grown + pltpu.roll(grown, 4, 0)
@@ -407,44 +446,47 @@
     owners = owner_map.reshape(-1, LANES)
     near0, near1 = swapped(crm_state, 0), swapped(crm_state, 1)
     tiles = capacity + capacity // 2
-    packed, picks = call(
-        pack_kernel,
-        (S((col_count * tiles, LANES), f32), S((capacity * col_count, columns), bf16)),
+    packed = call(pack_kernel, S((col_count * tiles, LANES), f32), (), 1, 3, 60)(
+        me, owners, profiles.T, courant.T
+    )
+    got = traded(packed.reshape(col_count, 1, tiles * LANES), "col").reshape(packed.shape)
+    chosen = S((capacity * col_count, columns), bf16)
+    lines = fields * levels
+    lands, picks, rate, start = call(
+        landing_kernel,
+        (chosen, chosen, S((2, 8, LANES), f32), S((lines, 8, LANES), f32)),
         (),
         1,
         3,
-        60,
-    )(me, owners, profiles.T, courant.T)
-    got = traded(packed.reshape(col_count, 1, tiles * LANES), "col").reshape(packed.shape)
-    lands = call(landing_kernel, S((capacity * col_count, columns), bf16), (), 1, 1)(me, owners)
+    )(me, owners, cloud_flags.reshape(1, columns), flat(crm_state))
     far0, far1 = swapped(near1, 0), swapped(near0, 1)
-    lines = fields * levels
     forces = call(
         forcing_kernel,
         (
             S((lines, 8, LANES), f32),
             S((levels, 8, LANES), f32),
             S((levels, 8, LANES), f32),
-            S((2, 8, LANES), f32),
         ),
         [pltpu.VMEM((lane_tiles, 3 * LANES // 2, LANES), f32)],
         0,
-        3,
-    )(got, lands, cloud_flags.reshape(1, columns))
+        2,
+    )(got, lands)
     parity = (lax.axis_index("grp") % 2).reshape(1)
-    own = flat(crm_state)
     state = pltpu.VMEM((lines, 40, LANES), f32)
-    edges = call(inner_kernel, S((6, lines, 8, LANES), f32), [state, state], 1, 7)(
-        parity, *forces, own, flat(near0), flat(near1)
+    edges = call(inner_kernel, S((5, lines, 8, LANES), f32), [state, state], 1, 7)(
+        parity, *forces, rate, start, flat(near0), flat(near1)
+    )
+    strip = call(side_kernel, S((lines, 8, LANES), f32), [state, state], 1, 6)(
+        parity, *forces, rate, flat(far0), edges
     )
     ended, change = call(
         outer_kernel,
-        (S(own.shape, f32), S((pieces, 2 * share, columns), f32)),
+        (S((lines, 8, LANES), f32), S((pieces, 2 * share, columns), f32)),
         [state, state, pltpu.VMEM((fields, lane_tiles, tall, LANES), f32)],
         1,
-        7,
-    )(parity, *forces, flat(far0), flat(far1), edges)
-    rows = call(finish_kernel, S(own.shape, f32), (), 0, 1)(ended)
+        8,
+    )(parity, *forces, rate, flat(far1), edges, strip, start)
+    rows = call(finish_kernel, S((lines, 8, LANES), f32), (), 0, 1)(ended)
     rows = rows.reshape(fields, levels, lane_tiles, cells, LANES).transpose(0, 1, 3, 2, 4)
     crm_final = rows.reshape(crm_state.shape)
     parts = traded(change, "grp")

time: 116 us -> 115 us (level)
  waiting for transfers between devices: 17.9 us -> 16 us
    all_to_all x2, waiting for transfers between devices: 17.9 us -> 15.9 us  [traded(): return lax.all_to_all(x, axis, split_axis=0, concat_axis=0, tiled=True)]
    pallas_call x5 -> x6, Pallas kernels: 11.9 us -> 12.7 us  [the longest x1 3.87 us: on_device(): call(outer_kernel, (S((lines, 8, LANES), f32), S((pieces, 2 * share, colu...]
    unnamed x8 -> x6, local copies, waits for them, and re-layouts: 2.54 us -> 2.54 us
  transfers between devices with their start and end apart: 6 -> 6, of which waited for: 2 -> 2; matrix products, arithmetic and copies ran while one was open for 0% -> 0% of each run, Pallas kernels for 7% -> 8%
where the time goes in v4:
time: 115 us; the launch traced here: 113 us
  starting transfers between devices  40.8 us (35%)
  blocking collectives  37.6 us (33%)
  waiting for transfers between devices  16 us (14%)
  Pallas kernels  15.6 us (14%)
  local copies, waits for them, and re-layouts  2.54 us (2%)
    all_to_all x2, blocking collectives, traded(): return lax.all_to_all(x, axis, split_axis=0, concat_axis=0, tiled=True)  37.6 us
    ppermute x4, starting transfers between devices, swapped(): lax.ppermute(x, 'grp', [(i, (i + 1 if i % 2 == odd else i - 1) % peers) f...  26.3 us
    all_to_all x2, waiting for transfers between devices, traded(): return lax.all_to_all(x, axis, split_axis=0, concat_axis=0, tiled=True)  15.9 us
    all_to_all x2, starting transfers between devices, traded(): return lax.all_to_all(x, axis, split_axis=0, concat_axis=0, tiled=True)  14.6 us
    pallas_call x1, Pallas kernels, on_device(): call(outer_kernel, (S((lines, 8, LANES), f32), S((pieces, 2 * share, colu...  3.87 us
    pallas_call x1, Pallas kernels, on_device(): call(inner_kernel, S((5, lines, 8, LANES), f32), [state, state], 1, 7)  3.42 us
    unnamed x6, local copies, waits for them, and re-layouts  2.54 us
  transfers between devices with their start and end apart: 6, of which 2 were waited for; matrix products, arithmetic and copies ran while one was open for 0% of the time, Pallas kernels for 8%

profile of v4, /device:TPU:1, one launch (start us, length us, event | category | flops | bytes accessed | tf_op | source)
XLA Modules:
  0.0 113.3 jit_solution(10636414535565670453)
XLA Ops:
  0.6 18.8 %collective-permute-start.2 = (f32[2,58,4,256]{3,2,1,0:T(4,128)}, f32[2,58,4,256]{3,2,1,0:T(4,128)S(1)}, u32[]{:S(2)}, u32[]{:S(2)}) collective-permute-start(f32[2,58,4,256]{3,2,1,0:T(4,128)} %param.9), channel_id=1, source_target_pairs={{0,15},{1,2},{2,1},{3,4},{4,3},{5,6},{6,5},{7,8},{8,7},{9,10},{10,... | collective-permute-start | bytes 1425416 | tf_op jit(solution)/shard_map/ppermute | solution.py:417
  19.4 1.9 %collective-permute-start = (f32[2,58,4,256]{3,2,1,0:T(4,128)}, f32[2,58,4,256]{3,2,1,0:T(4,128)S(1)}, u32[]{:S(2)}, u32[]{:S(2)}) collective-permute-start(f32[2,58,4,256]{3,2,1,0:T(4,128)} %param.9), channel_id=1, source_target_pairs={{0,1},{1,0},{2,3},{3,2},{4,5},{5,4},{6,7},{7,6},{8,9},{9,8},{10,11... | collective-permute-start | bytes 1425416 | tf_op jit(solution)/shard_map/ppermute | solution.py:417
  21.3 2.3 %shard_map.68 = f32[576,128]{1,0:T(8,128)} custom-call(s32[1]{0:T(128)} %bitcast.1.me, s32[128,128]{1,0:T(8,128)} %bitcast.49, f32[116,256]{1,0:T(8,128)} %bitcast.56, f32[58,256]{1,0:T(8,128)} %bitcast.58), custom_call_target="tpu_custom_call" | custom-call | tf_op jit(solution)/shard_map/pallas_call | solution.py:449
  23.6 11.1 %all-to-all-start = ((f32[64,1,1152]{2,1,0:T(1,128)}), f32[64,1,1152]{2,1,0:T(1,128)S(1)}, u32[]{:S(2)}, u32[]{:S(2)}) async-start(f32[64,1,1152]{2,1,0:T(1,128)} %bitcast.54), calls=%async_computation | async-start | bytes 589824 | tf_op jit(solution)/shard_map/all_to_all | solution.py:423
  34.7 0.0 collective-permute-done.2
  34.7 3.6 %collective-permute-start.3 = (f32[2,58,4,256]{3,2,1,0:T(4,128)S(1)}, f32[2,58,4,256]{3,2,1,0:T(4,128)S(1)}, u32[]{:S(2)}, u32[]{:S(2)}) collective-permute-start(f32[2,58,4,256]{3,2,1,0:T(4,128)S(1)} %collective-permute-done.2), channel_id=1, source_target_pairs={{0,1},{1,0},{2,3},{3,2},{4,5},{5,4},{6,7},{7,6},{8,9},{9,8},{10,11... | collective-permute-start | bytes 1425416 | tf_op jit(solution)/shard_map/ppermute | solution.py:417
  38.3 0.0 collective-permute-done
  38.3 1.9 %collective-permute-start.1 = (f32[2,58,4,256]{3,2,1,0:T(4,128)S(1)}, f32[2,58,4,256]{3,2,1,0:T(4,128)S(1)}, u32[]{:S(2)}, u32[]{:S(2)}) collective-permute-start(f32[2,58,4,256]{3,2,1,0:T(4,128)S(1)} %collective-permute-done), channel_id=1, source_target_pairs={{0,15},{1,2},{2,1},{3,4},{4,3},{5,6},{6,5},{7,8},{8,7},{9,10},{10,... | collective-permute-start | bytes 1425416 | tf_op jit(solution)/shard_map/ppermute | solution.py:417
  40.3 0.0 copy-start
  40.3 1.0 copy-done
  41.3 0.0 copy-start.1
  41.3 0.8 copy-done.1
  42.2 0.0 copy-start.2
  42.2 0.7 copy-done.2
  42.8 0.5 shard_map.69
  43.3 5.0 %all-to-all-done = f32[64,1,1152]{2,1,0:T(1,128)S(1)} async-done(((f32[64,1,1152]{2,1,0:T(1,128)}), f32[64,1,1152]{2,1,0:T(1,128)S(1)}, u32[]{:S(2)}, u32[]{:S(2)}) %all-to-all-start) | async-done | bytes 294944 | tf_op jit(solution)/shard_map/all_to_all | solution.py:423
  48.4 0.7 shard_map.70
  49.0 3.4 %shard_map.71.edges = f32[5,116,8,128]{3,2,1,0:T(8,128)S(1)} custom-call(s32[1]{0:T(128)} %bitcast.parity, f32[116,8,128]{2,1,0:T(8,128)S(1)} %get-tuple-element.12.force, f32[58,8,128]{2,1,0:T(8,128)S(1)} %get-tuple-element.13.east, f32[58,8,128]{2,1,0:T(8,128)S(1)} %get-tuple-element.14.west, f32[2,8,128]{2,1,0:T(8,128)S(1)} %get-tuple-element.15.rate, ...), custom_call_target="tpu_custom_call" | custom-call | tf_op jit(solution)/shard_map/pallas_call | solution.py:476
  52.5 0.0 collective-permute-done.3
  52.5 1.7 %shard_map.72.strip = f32[116,8,128]{2,1,0:T(8,128)S(1)} custom-call(s32[1]{0:T(128)} %bitcast.parity, f32[116,8,128]{2,1,0:T(8,128)S(1)} %get-tuple-element.12.force, f32[58,8,128]{2,1,0:T(8,128)S(1)} %get-tuple-element.13.east, f32[58,8,128]{2,1,0:T(8,128)S(1)} %get-tuple-element.14.west, f32[2,8,128]{2,1,0:T(8,128)S(1)} %get-tuple-element.15.rate, ...), custom_call_target="tpu_custom_call" | custom-call | tf_op jit(solution)/shard_map/pallas_call | solution.py:479
  54.2 0.0 collective-permute-done.1
  54.2 3.9 %shard_map.73 = (f32[116,8,128]{2,1,0:T(8,128)S(1)}, f32[16,8,256]{2,1,0:T(8,128)S(1)}) custom-call(s32[1]{0:T(128)} %bitcast.parity, f32[116,8,128]{2,1,0:T(8,128)S(1)} %get-tuple-element.12.force, f32[58,8,128]{2,1,0:T(8,128)S(1)} %get-tuple-element.13.east, f32[58,8,128]{2,1,0:T(8,128)S(1)} %get-tuple-element.14.west, ...), custom_call_target="tpu_custom_call" | custom-call | tf_op jit(solution)/shard_map/pallas_call | solution.py:482
  58.1 17.1 %all_to_all.20.parts = f32[16,8,256]{2,1,0:T(8,128)S(1)} all-to-all(f32[16,8,256]{2,1,0:T(8,128)S(1)} %get-tuple-element.17), channel_id=1, replica_groups=mesh['col'=64,'grp'=16] {'grp'}, dimensions={0} | all-to-all | bytes 262144 | tf_op jit(solution)/shard_map/all_to_all | solution.py:423
  75.2 0.3 shard_map.74
  75.5 20.5 %all_to_all.21 = f32[64,1,128]{2,1,0:T(1,128)S(1)} all-to-all(f32[64,1,128]{2,1,0:T(1,128)S(1)} %bitcast.51), channel_id=1, replica_groups=mesh['col'=64,'grp'=16] {'col'}, dimensions={0} | all-to-all | bytes 65536 | tf_op jit(solution)/shard_map/all_to_all | solution.py:423
  96.0 1.2 %shard_map.75 = f32[16,8,256]{2,1,0:T(8,128)} custom-call(f32[64,128]{1,0:T(8,128)S(1)} %bitcast.52, bf16[384,256]{1,0:T(8,128)(2,1)S(1)} %get-tuple-element.18.picks), custom_call_target="tpu_custom_call" | custom-call | tf_op jit(solution)/shard_map/pallas_call | solution.py:496
  97.2 3.5 %all-to-all-start.3 = ((f32[16,8,256]{2,1,0:T(8,128)}), f32[16,8,256]{2,1,0:T(8,128)S(1)}, u32[]{:S(2)}, u32[]{:S(2)}) async-start(f32[16,8,256]{2,1,0:T(8,128)} %shard_map.75), calls=%async_computation.3 | async-start | bytes 262144 | tf_op jit(solution)/shard_map/all_to_all | solution.py:423
  100.7 1.0 shard_map.77
  101.7 10.9 %all-to-all-done.3.every = f32[16,8,256]{2,1,0:T(8,128)S(1)} async-done(((f32[16,8,256]{2,1,0:T(8,128)}), f32[16,8,256]{2,1,0:T(8,128)S(1)}, u32[]{:S(2)}, u32[]{:S(2)}) %all-to-all-start.3) | async-done | bytes 131104 | tf_op jit(solution)/shard_map/all_to_all | solution.py:423
  112.6 0.7 shard_map.76
Async XLA Ops:
  0.6 34.0 %collective-permute-start.2 = (f32[2,58,4,256]{3,2,1,0:T(4,128)}, f32[2,58,4,256]{3,2,1,0:T(4,128)S(1)}, u32[]{:S(2)}, u32[]{:S(2)}) collective-permute-start(f32[2,58,4,256]{3,2,1,0:T(4,128)} %param.9), channel_id=1, source_target_pairs={{0,15},{1,2},{2,1},{3,4},{4,3},{5,6},{6,5},{7,8},{8,7},{9,10},{10,... | collective-permute-start | bytes 1425416 | tf_op jit(solution)/shard_map/ppermute | solution.py:417
  19.4 18.9 %collective-permute-start = (f32[2,58,4,256]{3,2,1,0:T(4,128)}, f32[2,58,4,256]{3,2,1,0:T(4,128)S(1)}, u32[]{:S(2)}, u32[]{:S(2)}) collective-permute-start(f32[2,58,4,256]{3,2,1,0:T(4,128)} %param.9), channel_id=1, source_target_pairs={{0,1},{1,0},{2,3},{3,2},{4,5},{5,4},{6,7},{7,6},{8,9},{9,8},{10,11... | collective-permute-start | bytes 1425416 | tf_op jit(solution)/shard_map/ppermute | solution.py:417
  23.6 24.8 %all-to-all-start = ((f32[64,1,1152]{2,1,0:T(1,128)}), f32[64,1,1152]{2,1,0:T(1,128)S(1)}, u32[]{:S(2)}, u32[]{:S(2)}) async-start(f32[64,1,1152]{2,1,0:T(1,128)} %bitcast.54), calls=%async_computation | async-start | bytes 589824 | tf_op jit(solution)/shard_map/all_to_all | solution.py:423
  34.7 17.8 %collective-permute-start.3 = (f32[2,58,4,256]{3,2,1,0:T(4,128)S(1)}, f32[2,58,4,256]{3,2,1,0:T(4,128)S(1)}, u32[]{:S(2)}, u32[]{:S(2)}) collective-permute-start(f32[2,58,4,256]{3,2,1,0:T(4,128)S(1)} %collective-permute-done.2), channel_id=1, source_target_pairs={{0,1},{1,0},{2,3},{3,2},{4,5},{5,4},{6,7},{7,6},{8,9},{9,8},{10,11... | collective-permute-start | bytes 1425416 | tf_op jit(solution)/shard_map/ppermute | solution.py:417
  38.3 15.8 %collective-permute-start.1 = (f32[2,58,4,256]{3,2,1,0:T(4,128)S(1)}, f32[2,58,4,256]{3,2,1,0:T(4,128)S(1)}, u32[]{:S(2)}, u32[]{:S(2)}) collective-permute-start(f32[2,58,4,256]{3,2,1,0:T(4,128)S(1)} %collective-permute-done), channel_id=1, source_target_pairs={{0,15},{1,2},{2,1},{3,4},{4,3},{5,6},{6,5},{7,8},{8,7},{9,10},{10,... | collective-permute-start | bytes 1425416 | tf_op jit(solution)/shard_map/ppermute | solution.py:417
  40.3 1.0 copy-start
  41.3 0.8 copy-start.1
  42.2 0.7 copy-start.2
  97.2 15.4 %all-to-all-start.3 = ((f32[16,8,256]{2,1,0:T(8,128)}), f32[16,8,256]{2,1,0:T(8,128)S(1)}, u32[]{:S(2)}, u32[]{:S(2)}) async-start(f32[16,8,256]{2,1,0:T(8,128)} %shard_map.75), calls=%async_computation.3 | async-start | bytes 262144 | tf_op jit(solution)/shard_map/all_to_all | solution.py:423

commit v5 on v4

--- a/solution.py
+++ b/solution.py
@@ -68,18 +68,17 @@
     chosen = chosen_slots(me, owners, peers, slots)
     gap = jnp.zeros((half - levels, columns), jnp.float32)
     wind = jnp.concatenate([cour[...], gap], axis=0)
-    blank = jnp.zeros_like(wind)
     table = jnp.concatenate(
-        [prof[...], jnp.zeros((LANES - feats, columns), jnp.float32), wind, blank, blank, wind],
-        axis=0,
+        [prof[...], jnp.zeros((LANES - feats, columns), jnp.float32), wind, wind], axis=0
     )
     rows = sum(dot(chosen, piece, ((1,), (1,))) for piece in thirds(table))
     for k in range(slots):
         packed[pl.ds(k, peers, stride=tiles), :] = rows[k * peers : (k + 1) * peers, :LANES]
+    first_half = lax.broadcasted_iota(jnp.int32, (peers, LANES), 1) < half
     for j in range(slots // 2):
         low = rows[2 * j * peers : (2 * j + 1) * peers, LANES : 2 * LANES]
-        high = rows[(2 * j + 1) * peers : (2 * j + 2) * peers, 2 * LANES :]
-        packed[pl.ds(slots + j, peers, stride=tiles), :] = low + high
+        high = rows[(2 * j + 1) * peers : (2 * j + 2) * peers, LANES : 2 * LANES]
+        packed[pl.ds(slots + j, peers, stride=tiles), :] = jnp.where(first_half, low, high)
 
 
 def landing_kernel(me, owners, flags, own, lands, picks, rate, start):

time: 115 us -> 115 us (level)
  no operation moved by 1% of the time
where the time goes in v5:
time: 115 us; the launch traced here: 113 us
  starting transfers between devices  40.8 us (35%)
  blocking collectives  37.6 us (33%)
  waiting for transfers between devices  16 us (14%)
  Pallas kernels  15.4 us (13%)
  local copies, waits for them, and re-layouts  2.54 us (2%)
    all_to_all x2, blocking collectives, traded(): return lax.all_to_all(x, axis, split_axis=0, concat_axis=0, tiled=True)  37.6 us
    ppermute x4, starting transfers between devices, swapped(): lax.ppermute(x, 'grp', [(i, (i + 1 if i % 2 == odd else i - 1) % peers) f...  26.2 us
    all_to_all x2, waiting for transfers between devices, traded(): return lax.all_to_all(x, axis, split_axis=0, concat_axis=0, tiled=True)  15.9 us
    all_to_all x2, starting transfers between devices, traded(): return lax.all_to_all(x, axis, split_axis=0, concat_axis=0, tiled=True)  14.6 us
    pallas_call x1, Pallas kernels, on_device(): call(outer_kernel, (S((lines, 8, LANES), f32), S((pieces, 2 * share, colu...  3.87 us
    pallas_call x1, Pallas kernels, on_device(): call(inner_kernel, S((5, lines, 8, LANES), f32), [state, state], 1, 7)  3.42 us
    unnamed x6, local copies, waits for them, and re-layouts  2.54 us
  transfers between devices with their start and end apart: 6, of which 2 were waited for; matrix products, arithmetic and copies ran while one was open for 0% of the time, Pallas kernels for 8%

profile of v5, /device:TPU:1, one launch (start us, length us, event | category | flops | bytes accessed | tf_op | source)
XLA Modules:
  0.0 113.1 jit_solution(16252194679298871880)
XLA Ops:
  0.6 18.8 %collective-permute-start.2 = (f32[2,58,4,256]{3,2,1,0:T(4,128)}, f32[2,58,4,256]{3,2,1,0:T(4,128)S(1)}, u32[]{:S(2)}, u32[]{:S(2)}) collective-permute-start(f32[2,58,4,256]{3,2,1,0:T(4,128)} %param.9), channel_id=1, source_target_pairs={{0,15},{1,2},{2,1},{3,4},{4,3},{5,6},{6,5},{7,8},{8,7},{9,10},{10,... | collective-permute-start | bytes 1425416 | tf_op jit(solution)/shard_map/ppermute | solution.py:416
  19.4 1.9 %collective-permute-start = (f32[2,58,4,256]{3,2,1,0:T(4,128)}, f32[2,58,4,256]{3,2,1,0:T(4,128)S(1)}, u32[]{:S(2)}, u32[]{:S(2)}) collective-permute-start(f32[2,58,4,256]{3,2,1,0:T(4,128)} %param.9), channel_id=1, source_target_pairs={{0,1},{1,0},{2,3},{3,2},{4,5},{5,4},{6,7},{7,6},{8,9},{9,8},{10,11... | collective-permute-start | bytes 1425416 | tf_op jit(solution)/shard_map/ppermute | solution.py:416
  21.3 2.1 %shard_map.68 = f32[576,128]{1,0:T(8,128)} custom-call(s32[1]{0:T(128)} %bitcast.1.me, s32[128,128]{1,0:T(8,128)} %bitcast.49, f32[116,256]{1,0:T(8,128)} %bitcast.56, f32[58,256]{1,0:T(8,128)} %bitcast.58), custom_call_target="tpu_custom_call" | custom-call | tf_op jit(solution)/shard_map/pallas_call | solution.py:448
  23.4 11.1 %all-to-all-start = ((f32[64,1,1152]{2,1,0:T(1,128)}), f32[64,1,1152]{2,1,0:T(1,128)S(1)}, u32[]{:S(2)}, u32[]{:S(2)}) async-start(f32[64,1,1152]{2,1,0:T(1,128)} %bitcast.54), calls=%async_computation | async-start | bytes 589824 | tf_op jit(solution)/shard_map/all_to_all | solution.py:422
  34.5 0.0 collective-permute-done.2
  34.5 3.6 %collective-permute-start.3 = (f32[2,58,4,256]{3,2,1,0:T(4,128)S(1)}, f32[2,58,4,256]{3,2,1,0:T(4,128)S(1)}, u32[]{:S(2)}, u32[]{:S(2)}) collective-permute-start(f32[2,58,4,256]{3,2,1,0:T(4,128)S(1)} %collective-permute-done.2), channel_id=1, source_target_pairs={{0,1},{1,0},{2,3},{3,2},{4,5},{5,4},{6,7},{7,6},{8,9},{9,8},{10,11... | collective-permute-start | bytes 1425416 | tf_op jit(solution)/shard_map/ppermute | solution.py:416
  38.2 0.0 collective-permute-done
  38.2 1.9 %collective-permute-start.1 = (f32[2,58,4,256]{3,2,1,0:T(4,128)S(1)}, f32[2,58,4,256]{3,2,1,0:T(4,128)S(1)}, u32[]{:S(2)}, u32[]{:S(2)}) collective-permute-start(f32[2,58,4,256]{3,2,1,0:T(4,128)S(1)} %collective-permute-done), channel_id=1, source_target_pairs={{0,15},{1,2},{2,1},{3,4},{4,3},{5,6},{6,5},{7,8},{8,7},{9,10},{10,... | collective-permute-start | bytes 1425416 | tf_op jit(solution)/shard_map/ppermute | solution.py:416
  40.1 0.0 copy-start
  40.1 1.0 copy-done
  41.2 0.0 copy-start.1
  41.2 0.8 copy-done.1
  42.0 0.0 copy-start.2
  42.0 0.7 copy-done.2
  42.7 0.5 shard_map.69
  43.2 5.0 %all-to-all-done = f32[64,1,1152]{2,1,0:T(1,128)S(1)} async-done(((f32[64,1,1152]{2,1,0:T(1,128)}), f32[64,1,1152]{2,1,0:T(1,128)S(1)}, u32[]{:S(2)}, u32[]{:S(2)}) %all-to-all-start) | async-done | bytes 294944 | tf_op jit(solution)/shard_map/all_to_all | solution.py:422
  48.2 0.7 shard_map.70
  48.9 3.4 %shard_map.71.edges = f32[5,116,8,128]{3,2,1,0:T(8,128)S(1)} custom-call(s32[1]{0:T(128)} %bitcast.parity, f32[116,8,128]{2,1,0:T(8,128)S(1)} %get-tuple-element.12.force, f32[58,8,128]{2,1,0:T(8,128)S(1)} %get-tuple-element.13.east, f32[58,8,128]{2,1,0:T(8,128)S(1)} %get-tuple-element.14.west, f32[2,8,128]{2,1,0:T(8,128)S(1)} %get-tuple-element.15.rate, ...), custom_call_target="tpu_custom_call" | custom-call | tf_op jit(solution)/shard_map/pallas_call | solution.py:475
  52.3 0.0 collective-permute-done.3
  52.3 1.7 %shard_map.72.strip = f32[116,8,128]{2,1,0:T(8,128)S(1)} custom-call(s32[1]{0:T(128)} %bitcast.parity, f32[116,8,128]{2,1,0:T(8,128)S(1)} %get-tuple-element.12.force, f32[58,8,128]{2,1,0:T(8,128)S(1)} %get-tuple-element.13.east, f32[58,8,128]{2,1,0:T(8,128)S(1)} %get-tuple-element.14.west, f32[2,8,128]{2,1,0:T(8,128)S(1)} %get-tuple-element.15.rate, ...), custom_call_target="tpu_custom_call" | custom-call | tf_op jit(solution)/shard_map/pallas_call | solution.py:478
  54.0 0.0 collective-permute-done.1
  54.0 3.9 %shard_map.73 = (f32[116,8,128]{2,1,0:T(8,128)S(1)}, f32[16,8,256]{2,1,0:T(8,128)S(1)}) custom-call(s32[1]{0:T(128)} %bitcast.parity, f32[116,8,128]{2,1,0:T(8,128)S(1)} %get-tuple-element.12.force, f32[58,8,128]{2,1,0:T(8,128)S(1)} %get-tuple-element.13.east, f32[58,8,128]{2,1,0:T(8,128)S(1)} %get-tuple-element.14.west, ...), custom_call_target="tpu_custom_call" | custom-call | tf_op jit(solution)/shard_map/pallas_call | solution.py:481
  57.9 17.1 %all_to_all.20.parts = f32[16,8,256]{2,1,0:T(8,128)S(1)} all-to-all(f32[16,8,256]{2,1,0:T(8,128)S(1)} %get-tuple-element.17), channel_id=1, replica_groups=mesh['col'=64,'grp'=16] {'grp'}, dimensions={0} | all-to-all | bytes 262144 | tf_op jit(solution)/shard_map/all_to_all | solution.py:422
  75.0 0.3 shard_map.74
  75.4 20.5 %all_to_all.21 = f32[64,1,128]{2,1,0:T(1,128)S(1)} all-to-all(f32[64,1,128]{2,1,0:T(1,128)S(1)} %bitcast.51), channel_id=1, replica_groups=mesh['col'=64,'grp'=16] {'col'}, dimensions={0} | all-to-all | bytes 65536 | tf_op jit(solution)/shard_map/all_to_all | solution.py:422
  95.9 1.2 %shard_map.75 = f32[16,8,256]{2,1,0:T(8,128)} custom-call(f32[64,128]{1,0:T(8,128)S(1)} %bitcast.52, bf16[384,256]{1,0:T(8,128)(2,1)S(1)} %get-tuple-element.18.picks), custom_call_target="tpu_custom_call" | custom-call | tf_op jit(solution)/shard_map/pallas_call | solution.py:495
  97.0 3.5 %all-to-all-start.3 = ((f32[16,8,256]{2,1,0:T(8,128)}), f32[16,8,256]{2,1,0:T(8,128)S(1)}, u32[]{:S(2)}, u32[]{:S(2)}) async-start(f32[16,8,256]{2,1,0:T(8,128)} %shard_map.75), calls=%async_computation.3 | async-start | bytes 262144 | tf_op jit(solution)/shard_map/all_to_all | solution.py:422
  100.5 1.0 shard_map.77
  101.5 10.9 %all-to-all-done.3.every = f32[16,8,256]{2,1,0:T(8,128)S(1)} async-done(((f32[16,8,256]{2,1,0:T(8,128)}), f32[16,8,256]{2,1,0:T(8,128)S(1)}, u32[]{:S(2)}, u32[]{:S(2)}) %all-to-all-start.3) | async-done | bytes 131104 | tf_op jit(solution)/shard_map/all_to_all | solution.py:422
  112.5 0.7 shard_map.76
Async XLA Ops:
  0.6 33.9 %collective-permute-start.2 = (f32[2,58,4,256]{3,2,1,0:T(4,128)}, f32[2,58,4,256]{3,2,1,0:T(4,128)S(1)}, u32[]{:S(2)}, u32[]{:S(2)}) collective-permute-start(f32[2,58,4,256]{3,2,1,0:T(4,128)} %param.9), channel_id=1, source_target_pairs={{0,15},{1,2},{2,1},{3,4},{4,3},{5,6},{6,5},{7,8},{8,7},{9,10},{10,... | collective-permute-start | bytes 1425416 | tf_op jit(solution)/shard_map/ppermute | solution.py:416
  19.4 18.8 %collective-permute-start = (f32[2,58,4,256]{3,2,1,0:T(4,128)}, f32[2,58,4,256]{3,2,1,0:T(4,128)S(1)}, u32[]{:S(2)}, u32[]{:S(2)}) collective-permute-start(f32[2,58,4,256]{3,2,1,0:T(4,128)} %param.9), channel_id=1, source_target_pairs={{0,1},{1,0},{2,3},{3,2},{4,5},{5,4},{6,7},{7,6},{8,9},{9,8},{10,11... | collective-permute-start | bytes 1425416 | tf_op jit(solution)/shard_map/ppermute | solution.py:416
  23.4 24.8 %all-to-all-start = ((f32[64,1,1152]{2,1,0:T(1,128)}), f32[64,1,1152]{2,1,0:T(1,128)S(1)}, u32[]{:S(2)}, u32[]{:S(2)}) async-start(f32[64,1,1152]{2,1,0:T(1,128)} %bitcast.54), calls=%async_computation | async-start | bytes 589824 | tf_op jit(solution)/shard_map/all_to_all | solution.py:422
  34.5 17.8 %collective-permute-start.3 = (f32[2,58,4,256]{3,2,1,0:T(4,128)S(1)}, f32[2,58,4,256]{3,2,1,0:T(4,128)S(1)}, u32[]{:S(2)}, u32[]{:S(2)}) collective-permute-start(f32[2,58,4,256]{3,2,1,0:T(4,128)S(1)} %collective-permute-done.2), channel_id=1, source_target_pairs={{0,1},{1,0},{2,3},{3,2},{4,5},{5,4},{6,7},{7,6},{8,9},{9,8},{10,11... | collective-permute-start | bytes 1425416 | tf_op jit(solution)/shard_map/ppermute | solution.py:416
  38.2 15.8 %collective-permute-start.1 = (f32[2,58,4,256]{3,2,1,0:T(4,128)S(1)}, f32[2,58,4,256]{3,2,1,0:T(4,128)S(1)}, u32[]{:S(2)}, u32[]{:S(2)}) collective-permute-start(f32[2,58,4,256]{3,2,1,0:T(4,128)S(1)} %collective-permute-done), channel_id=1, source_target_pairs={{0,15},{1,2},{2,1},{3,4},{4,3},{5,6},{6,5},{7,8},{8,7},{9,10},{10,... | collective-permute-start | bytes 1425416 | tf_op jit(solution)/shard_map/ppermute | solution.py:416
  40.1 1.0 copy-start
  41.2 0.8 copy-start.1
  42.0 0.7 copy-start.2
  97.0 15.4 %all-to-all-start.3 = ((f32[16,8,256]{2,1,0:T(8,128)}), f32[16,8,256]{2,1,0:T(8,128)S(1)}, u32[]{:S(2)}, u32[]{:S(2)}) async-start(f32[16,8,256]{2,1,0:T(8,128)} %shard_map.75), calls=%async_computation.3 | async-start | bytes 262144 | tf_op jit(solution)/shard_map/all_to_all | solution.py:422
